TPU v7x, 32 devices: a whole 2x2x4 slice. The times are simulated.
32 devices in a mesh: batch: 8 (over z, x), chan: 4 (over y, core).
Axes of the slice: x: 2, y: 2, z: 4, core: 2. Of those that a mesh axis runs over, the one named last changes fastest.
Arguments:
- signal: float32 [1024, 32768], P('chan', 'batch'), may hold values from -6 to 6
- cotangent: float32 [1024, 32768], P('chan', 'batch'), may hold values from -6 to 6
- first_layer: float32 [33, 64], replicated, may hold values from -5 to 5
- second_layer: float32 [64, 1024], P(None, 'chan'), may hold values from -0.75 to 0.75
- decay_rate: float32 [1024], P('chan'), may hold values from 0.3 to 600
- skip_gain: float32 [1024], P('chan'), may hold values from -4 to 4
Outputs:
- input_grad: float32 [1024, 32768], P('chan', 'batch')
- first_grad: float32 [33, 64], replicated
- second_grad: float32 [64, 1024], P(None, 'chan')
- decay_grad: float32 [1024], P('chan')
- skip_grad: float32 [1024], P('chan')
All inputs are finite; a program needn't handle non-finite values.
Results may differ from a plain program's by a relative error of at most 0.0003.
Values sent between devices are 32-bit elements; how exact they have to be, the bound alone decides.
A program may use at most 256 MiB of HBM per device.

v0:
```python
import functools
import math

import jax
import jax.numpy as jnp
import numpy as np
from jax import lax
from jax.experimental import pallas as pl
from jax.experimental.pallas import tpu as pltpu
from jax.sharding import PartitionSpec as P

COLS = 256

exact = lax.Precision.HIGHEST
precise = lax.Precision.HIGH
epsilon = 1e-06


def sincos(x):
    turns = jnp.round(x * (2.0 / math.pi))
    r = x - turns * 1.5703125
    r = r - turns * 4.837512969970703125e-4
    r = r - turns * 7.549789948768648e-8
    sq = r * r
    sine = r + r * sq * (-1.6666654611e-1 + sq * (8.3321608736e-3 + sq * -1.9515295891e-4))
    cosine = 1.0 - 0.5 * sq + sq * sq * (
        4.166664568298827e-2 + sq * (-1.388731625493765e-3 + sq * 2.443315711809948e-5)
    )
    quadrant = turns.astype(jnp.int32) & 3
    odd = (quadrant & 1) == 1
    sin_value = jnp.where(odd, cosine, sine)
    cos_value = jnp.where(odd, sine, cosine)
    sin_value = jnp.where(quadrant >= 2, -sin_value, sin_value)
    cos_value = jnp.where((quadrant == 1) | (quadrant == 2), -cos_value, cos_value)
    return sin_value, cos_value


def features(positions, length, band_count):
    band_index = jnp.arange(1, band_count + 1, dtype=jnp.int32)
    phase = (band_index[:, None] * positions[None, :] % length).astype(jnp.float32) * (
        2.0 * math.pi / length
    )
    linear = positions.astype(jnp.float32)[None, :] / length
    sines, cosines = sincos(phase)
    return jnp.concatenate([linear, cosines, sines], axis=0)


def pair(matrix):
    high = matrix.astype(np.float32).astype(jnp.bfloat16)
    low = (matrix - high.astype(np.float64)).astype(np.float32).astype(jnp.bfloat16)
    return jnp.asarray(high), jnp.asarray(low)


def tables(rows, cols):
    r = np.arange(rows, dtype=np.float64)
    c = np.arange(cols, dtype=np.float64)
    first = 2.0 * np.pi * np.outer(r + 0.5, r) / (2 * rows)
    twist = 2.0 * np.pi * np.outer(r + 0.5, c) / (2 * rows * cols)
    angle = 2.0 * np.pi * (np.outer(c, c) % cols) / cols
    cos_c, sin_c = np.cos(angle), np.sin(angle)
    stage1 = np.concatenate([np.cos(first), -np.sin(first)], axis=0)
    stage2 = np.block([[cos_c, -sin_c], [sin_c, cos_c]])
    last = np.concatenate([np.cos(first.T), -np.sin(first.T)], axis=1) / (rows * cols)
    return (
        *pair(stage1),
        *pair(stage2),
        *pair(stage2.T.copy()),
        *pair(last),
        jnp.asarray(np.cos(twist), jnp.float32),
        jnp.asarray(np.sin(twist), jnp.float32),
    )


def split(x):
    high = x.astype(jnp.bfloat16)
    return high, (x - high.astype(jnp.float32)).astype(jnp.bfloat16)


def dot(a, b):
    return jnp.dot(a, b, preferred_element_type=jnp.float32)


def product(left, right):
    return dot(left[0], right[0]) + (dot(left[1], right[0]) + dot(left[0], right[1]))


def kernel(count, val, cot, filt, w1h, w1l, w2h, w2l, w3h, w3l, w4h, w4l, ct, st, out_in, out_filt):
    rows, cols = ct.shape
    cos_t, sin_t = ct[...], st[...]
    first = (w1h[...], w1l[...])
    for c in range(count):
        parts = []
        for ref in (val, cot, filt):
            t = product(first, split(ref[c]))
            re, im = t[:rows], t[rows:]
            parts.append(
                jnp.concatenate([re * cos_t + im * sin_t, im * cos_t - re * sin_t], axis=1)
            )
        spec = product(split(jnp.concatenate(parts, axis=0)), (w2h[...], w2l[...]))
        v_re, v_im = spec[:rows, :cols], spec[:rows, cols:]
        c_re, c_im = spec[rows : 2 * rows, :cols], spec[rows : 2 * rows, cols:]
        f_re, f_im = spec[2 * rows :, :cols], spec[2 * rows :, cols:]
        prods = jnp.concatenate(
            [
                jnp.concatenate([f_re * c_re + f_im * c_im, f_re * c_im - f_im * c_re], axis=1),
                jnp.concatenate([v_re * c_re + v_im * c_im, v_re * c_im - v_im * c_re], axis=1),
            ],
            axis=0,
        )
        back = product(split(prods), (w3h[...], w3l[...]))
        for i, out in enumerate((out_in, out_filt)):
            re, im = back[i * rows : (i + 1) * rows, :cols], back[i * rows : (i + 1) * rows, cols:]
            turn = jnp.concatenate([re * cos_t - im * sin_t, im * cos_t + re * sin_t], axis=0)
            out[c] = product((w4h[...], w4l[...]), split(turn))


def correlate(values, cotan, filt):
    channels, rows, cols = values.shape
    count = 2 if channels % 2 == 0 else 1
    tabs = tables(rows, cols)
    block = pl.BlockSpec((count, rows, cols), lambda i: (i, 0, 0))
    shape = jax.ShapeDtypeStruct(values.shape, jnp.float32)
    flops = 2 * 3 * channels * rows * cols * (5 * 2 * rows + 5 * 4 * cols)
    return pl.pallas_call(
        functools.partial(kernel, count),
        grid=(channels // count,),
        in_specs=[block] * 3 + [pl.BlockSpec(t.shape, lambda i: (0, 0)) for t in tabs],
        out_specs=[block, block],
        out_shape=[shape, shape],
        compiler_params=pltpu.CompilerParams(vmem_limit_bytes=56 * 1024 * 1024),
        cost_estimate=pl.CostEstimate(
            flops=flops, bytes_accessed=5 * 4 * values.size, transcendentals=0
        ),
        name="correlate",
    )(values, cotan, filt, *tabs)


def local(signal, cotangent, first_layer, second_layer, decay_rate, skip_gain):
    groups = lax.axis_size("batch")
    place = lax.axis_index("batch")
    width_dev, local_len = signal.shape
    length = local_len * groups
    cols = COLS
    factor = 1.0 / math.sqrt(length)
    narrow = width_dev // groups

    def spread(x):
        x = x.reshape(width_dev, local_len // cols, cols)
        return lax.all_to_all(x, "batch", split_axis=0, concat_axis=1, tiled=True)

    val, cot = spread(signal), spread(cotangent)
    positions = jnp.arange(length, dtype=jnp.int32)
    columns = lax.dynamic_slice_in_dim(second_layer, place * narrow, narrow, 1)
    rates = lax.dynamic_slice_in_dim(decay_rate, place * narrow, narrow, 0)
    gains = lax.dynamic_slice_in_dim(skip_gain, place * narrow, narrow, 0)
    embed = features(positions, length, first_layer.shape[0] // 2)
    before = jnp.dot(first_layer.T, embed, precision=exact)
    basis, slope = sincos(before)
    fraction = positions.astype(jnp.float32) / length
    window = jnp.exp(-rates[:, None] * fraction[None, :])
    shaped = window * jnp.dot(columns.T, basis, precision=precise)
    norms = jnp.sqrt(jnp.sum(shaped * shaped, axis=1, keepdims=True) + epsilon)
    filt = shaped / norms
    taps = filt + jnp.where(positions[None, :] == 0, gains[:, None], 0.0)
    in_grad, filt_grad = correlate(val, cot, taps.reshape(val.shape))
    input_grad = lax.all_to_all(in_grad, "batch", split_axis=1, concat_axis=0, tiled=True)
    input_grad = input_grad.reshape(width_dev, local_len)
    dfilt = factor * filt_grad.reshape(narrow, length)
    skip_part = factor * jnp.sum(cot * val, axis=(1, 2))
    project = jnp.sum(filt * dfilt, axis=1, keepdims=True)
    draw = (dfilt - filt * project) / norms
    decay_part = -jnp.sum(draw * shaped * fraction[None, :], axis=1)
    dmix = draw * window
    second_part = jnp.dot(basis, dmix.T, precision=precise)
    dbasis = jnp.dot(columns, dmix, precision=precise)
    first_part = jnp.dot(embed, (slope * dbasis).T, precision=precise)
    second_grad, decay_grad, skip_grad = (
        lax.all_gather(second_part, "batch", axis=1, tiled=True),
        lax.all_gather(decay_part, "batch", axis=0, tiled=True),
        lax.all_gather(skip_part, "batch", axis=0, tiled=True),
    )
    first_grad = lax.psum(first_part, ("batch", "chan"))
    return (input_grad, first_grad, second_grad, decay_grad, skip_grad)


def solution(mesh):
    placed = (P("chan", "batch"), P("chan", "batch"), P(), P(None, "chan"), P("chan"), P("chan"))
    return jax.shard_map(
        local,
        mesh=mesh,
        in_specs=placed,
        out_specs=(P("chan", "batch"), P(), P(None, "chan"), P("chan"), P("chan")),
        check_vma=False,
    )
```

profile of v0, /device:TPU:0, one launch (start us, length us, event | category | flops | bytes accessed | tf_op | source)
XLA Modules:
  0.0 513.4 jit_solution(4661517701150644483)
XLA Ops:
  0.6 6.0 %copy.32 = f32[32,8,16,256]{3,2,1,0:T(8,128)} copy(f32[32,8,16,256]{3,1,2,0:T(8,128)} %bitcast.38) | data formatting | bytes 8388608
  6.6 7.3 %all-to-all-start = ((f32[256,16,256]{2,1,0:T(8,128)}), f32[256,16,256]{2,1,0:T(8,128)}, u32[]{:S(2)}, u32[]{:S(2)}) async-start(f32[256,16,256]{2,1,0:T(8,128)} %bitcast.33), calls=%async_computation | async-start | bytes 8388608 | tf_op jit(solution)/shard_map/all_to_all | solution.py:149
  13.9 4.8 negate_select_fusion.3
  18.7 3.7 copy.33
  22.7 19.2 %negate_select_fusion.1 = (f32[64,32768]{1,0:T(8,128)S(1)}, f32[64,32768]{1,0:T(8,128)}) fusion(f32[33,64]{1,0:T(8,128)S(1)} %copy-done.6, f32[16,32768]{1,0:T(8,128)} %get-tuple-element.29, f32[16,32768]{1,0:T(8,128)S(1)} %get-tuple-element.28, f32[1,32768]{1,0:T(1,128)S(1)} %convert_multiply_fusion), kind=kOutput, calls=%fused_computation.4 | convolution fusion | flops 901840896 | bytes 21111040 | tf_op jit(solution)/shard_map/dot_general | solution.py:157
  41.9 5.0 multiply_reduce_fusion.3
  46.9 60.2 %all-to-all-done = f32[256,16,256]{2,1,0:T(8,128)} async-done(((f32[256,16,256]{2,1,0:T(8,128)}), f32[256,16,256]{2,1,0:T(8,128)}, u32[]{:S(2)}, u32[]{:S(2)}) %all-to-all-start) | async-done | bytes 4194336 | tf_op jit(solution)/shard_map/all_to_all | solution.py:149
  107.2 4.7 all-to-all-start.1
  111.9 2.7 select_add_fusion
  114.7 3.4 copy.34
  118.0 4.8 copy.27
  122.9 81.6 %all-to-all-done.1 = f32[256,16,256]{2,1,0:T(8,128)} async-done(((f32[256,16,256]{2,1,0:T(8,128)}), f32[256,16,256]{2,1,0:T(8,128)}, u32[]{:S(2)}, u32[]{:S(2)}) %all-to-all-start.1) | async-done | bytes 4194336 | tf_op jit(solution)/shard_map/all_to_all | solution.py:149
  204.5 4.7 copy.28
  209.2 87.1 %correlate.1 = (f32[32,128,256]{2,1,0:T(8,128)}, f32[32,128,256]{2,1,0:T(8,128)}) custom-call(f32[32,128,256]{2,1,0:T(8,128)} %bitcast.41, f32[32,128,256]{2,1,0:T(8,128)} %bitcast.42, f32[32,128,256]{2,1,0:T(8,128)} %bitcast.40, bf16[256,128]{1,0:T(8,128)(2,1)} %constant.31.clone.w1h, bf16[256,128]{1,0:T(8,128)(2,1)} %constant.32.clone.w1l, ...), custom_call_target="tpu_custom_call" | custom-call | flops 40265318400 | bytes 20971520 | tf_op jit(solution)/shard_map/correlate/pallas_call | solution.py:124
  296.4 6.6 %copy.29 = f32[32,128,256]{2,0,1:T(8,128)} copy(f32[32,128,256]{2,1,0:T(8,128)} %get-tuple-element.7) | data formatting | bytes 8388608 | tf_op jit(solution)/shard_map/correlate/pallas_call | solution.py:124
  303.0 4.9 all-to-all-start.2
  307.9 0.6 dynamic-slice
  309.2 2.6 broadcast_multiply_fusion
  311.8 2.4 copy.36
  314.2 0.9 multiply_reduce_fusion.2
  315.1 1.5 multiply_reduce_fusion.1
  316.7 1.2 slice-done.1
  317.9 3.9 fusion.11
  321.8 98.6 %all_gather.9 = f32[64,256]{0,1:T(8,128)S(1)} all-gather(f32[64,32]{0,1:T(8,128)S(1)} %fusion.11), channel_id=1, replica_groups=mesh['batch'=8,'chan'=4] {'batch'}, dimensions={1}, use_global_device_ids=true | all-gather | bytes 73728 | tf_op jit(solution)/shard_map/all_gather | solution.py:178
  420.5 0.7 copy.31
  421.2 4.1 multiply_reduce_fusion
  425.4 20.3 %all-reduce.2 = (f32[256]{0:T(256)}, f32[256]{0:T(256)}) all-reduce(f32[256]{0:T(256)S(1)} %negate_dynamic-update-slice_fusion, f32[256]{0:T(256)S(1)} %multiply_dynamic-update-slice_fusion), channel_id=1, replica_groups=mesh['batch'=8,'chan'=4] {'batch'}, use_global_device_ids=true, to_apply=%add | all-reduce | flops 512 | bytes 4096
  445.7 15.5 %convolution_multiply_fusion = f32[64,32768]{1,0:T(8,128)S(1)} fusion(f32[64,32768]{1,0:T(8,128)} %get-tuple-element.31, f32[32,32768]{1,0:T(8,128)} %copy-done.3, f32[32768]{0:T(1024)S(1)} %convert_multiply_fusion.1, f32[32]{0:T(128)S(1)} %dynamic-slice_negate_fusion, f32[64,256]{1,0:T(8,128)S(1)} %copy-done, s32[]{:T(128)S(6)} %select_n.44), kind=kOutput, calls=%fused_computation | convolution fusion | flops 480247808 | bytes 21135876 | tf_op jit(solution)/shard_map/dot_general | solution.py:175
  461.2 3.7 fusion.10
  464.9 37.6 %psum.7 = f32[33,64]{1,0:T(8,128)} all-reduce(f32[33,64]{1,0:T(8,128)S(1)} %fusion.10), channel_id=1, replica_groups=mesh['batch'=8,'chan'=4] {'batch','chan'}, use_global_device_ids=true, to_apply=%region_2.3 | all-reduce | flops 2112 | bytes 16896 | tf_op jit(solution)/shard_map/psum | solution.py:182
  502.5 4.6 copy.30
  507.1 5.8 %copy.35 = f32[32,8,16,256]{3,1,2,0:T(8,128)} copy(f32[32,8,16,256]{3,2,1,0:T(8,128)S(1)} %bitcast.37) | data formatting | bytes 8388608
  (36 shorter events, 0.5 us)
Async XLA Ops:
  0.6 41.2 %copy-start = (f32[64,256]{1,0:T(8,128)S(1)}, f32[64,256]{1,0:T(8,128)}, u32[]{:S(2)}) copy-start(f32[64,256]{1,0:T(8,128)} %param.19) | copy-start | bytes 196612
  6.6 100.6 %all-to-all-start = ((f32[256,16,256]{2,1,0:T(8,128)}), f32[256,16,256]{2,1,0:T(8,128)}, u32[]{:S(2)}, u32[]{:S(2)}) async-start(f32[256,16,256]{2,1,0:T(8,128)} %bitcast.33), calls=%async_computation | async-start | bytes 8388608 | tf_op jit(solution)/shard_map/all_to_all | solution.py:149
  13.9 4.8 copy-start.5
  18.7 3.7 copy-start.7
  18.7 3.7 copy-start.8
  18.7 4.0 copy-start.6
  41.9 5.0 copy-start.2
  107.2 97.3 %all-to-all-start.1 = ((f32[256,16,256]{2,1,0:T(8,128)}), f32[256,16,256]{2,1,0:T(8,128)}, u32[]{:S(2)}, u32[]{:S(2)}) async-start(f32[256,16,256]{2,1,0:T(8,128)} %bitcast.34), calls=%async_computation.1 | async-start | bytes 8388608 | tf_op jit(solution)/shard_map/all_to_all | solution.py:149
  303.0 4.9 copy-start.9
  303.0 199.5 %all-to-all-start.2 = ((f32[32,128,256]{2,0,1:T(8,128)}), f32[32,128,256]{2,0,1:T(8,128)}, u32[]{:S(2)}, u32[]{:S(2)}) async-start(f32[32,128,256]{2,0,1:T(8,128)} %copy.29), calls=%async_computation.2 | async-start | bytes 8388608 | tf_op jit(solution)/shard_map/all_to_all | solution.py:166
  311.7 2.4 copy-start.1
  314.2 2.5 slice-start
  315.1 2.8 slice-start.1
  316.7 5.2 %copy-start.3 = (f32[32,32768]{1,0:T(8,128)}, f32[32,32768]{1,0:T(8,128)S(1)}, u32[]{:S(2)}) copy-start(f32[32,32768]{1,0:T(8,128)S(1)} %get-tuple-element.27) | copy-start | bytes 12582916
  445.7 15.5 %copy-start.4 = (f32[16,32768]{1,0:T(8,128)S(1)}, f32[16,32768]{1,0:T(8,128)}, u32[]{:S(2)}) copy-start(f32[16,32768]{1,0:T(8,128)} %get-tuple-element.29) | copy-start | bytes 6291460
where the time goes:
time: 524 us; the launch traced here: 513 us
  blocking collectives  157 us (30%)
  waiting for transfers between devices  142 us (27%)
  Pallas kernels  87.1 us (17%)
  matrix products  47.3 us (9%)
  local copies, waits for them, and re-layouts  44.7 us (9%)
  other arithmetic  17 us (3%)
  starting transfers between devices  16.9 us (3%)
    all_to_all x2, waiting for transfers between devices, spread(): return lax.all_to_all(x, 'batch', split_axis=0, concat_axis=1, tiled=True)  142 us
    all_gather x1, blocking collectives, local(): lax.all_gather(second_part, 'batch', axis=1, tiled=True)  98.6 us
    pallas_call x1, Pallas kernels, correlate(): pl.pallas_call(functools.partial(kernel, count), grid=(channels // count,...  87.1 us
    psum x1, blocking collectives, local(): first_grad = lax.psum(first_part, ('batch', 'chan'))  37.6 us
    unnamed x33, local copies, waits for them, and re-layouts  23.8 us
    unnamed x1, blocking collectives  20.3 us
    dot_general x1, matrix products, local(): before = jnp.dot(first_layer.T, embed, precision=exact)  19.2 us
    dot_general x1, matrix products, local(): dbasis = jnp.dot(columns, dmix, precision=precise)  15.5 us
  transfers between devices with their start and end apart: 3, of which 2 were waited for; matrix products, arithmetic and copies ran while one was open for 16% of the time, Pallas kernels for 0%

commit v1 on v0

v1 whole, which is shorter than its diff:
```python
import functools
import math

import jax
import jax.numpy as jnp
import numpy as np
from jax import lax
from jax.experimental import pallas as pl
from jax.experimental.pallas import tpu as pltpu
from jax.sharding import PartitionSpec as P

LANES = 128

exact = lax.Precision.HIGHEST
precise = lax.Precision.HIGH
epsilon = 1e-06


def sincos(x):
    turns = jnp.round(x * (2.0 / math.pi))
    r = x - turns * 1.5703125
    r = r - turns * 4.837512969970703125e-4
    r = r - turns * 7.549789948768648e-8
    sq = r * r
    sine = r + r * sq * (-1.6666654611e-1 + sq * (8.3321608736e-3 + sq * -1.9515295891e-4))
    cosine = 1.0 - 0.5 * sq + sq * sq * (
        4.166664568298827e-2 + sq * (-1.388731625493765e-3 + sq * 2.443315711809948e-5)
    )
    quadrant = turns.astype(jnp.int32) & 3
    odd = (quadrant & 1) == 1
    sin_value = jnp.where(odd, cosine, sine)
    cos_value = jnp.where(odd, sine, cosine)
    sin_value = jnp.where(quadrant >= 2, -sin_value, sin_value)
    cos_value = jnp.where((quadrant == 1) | (quadrant == 2), -cos_value, cos_value)
    return sin_value, cos_value


def features(positions, length, band_count):
    band_index = jnp.arange(1, band_count + 1, dtype=jnp.int32)
    phase = (band_index[:, None] * positions[None, :] % length).astype(jnp.float32) * (
        2.0 * math.pi / length
    )
    linear = positions.astype(jnp.float32)[None, :] / length
    sines, cosines = sincos(phase)
    return jnp.concatenate([linear, cosines, sines], axis=0)


def pair(matrix):
    high = matrix.astype(np.float32).astype(jnp.bfloat16)
    low = (matrix - high.astype(np.float64)).astype(np.float32).astype(jnp.bfloat16)
    return jnp.asarray(high), jnp.asarray(low)


def tables(rows, cols):
    r = np.arange(rows, dtype=np.float64)
    c = np.arange(cols, dtype=np.float64)
    first = 2.0 * np.pi * np.outer(r + 0.5, r) / (2 * rows)
    twist = 2.0 * np.pi * np.outer(r + 0.5, c) / (2 * rows * cols)
    angle = 2.0 * np.pi * (np.outer(c, c) % cols) / cols
    cos_c, sin_c = np.cos(angle), np.sin(angle)
    stage1 = np.concatenate([np.cos(first), -np.sin(first)], axis=0)
    stage2 = np.block([[cos_c, -sin_c], [sin_c, cos_c]])
    last = np.concatenate([np.cos(first.T), -np.sin(first.T)], axis=1) / (rows * cols)
    return (
        *pair(stage1),
        *pair(stage2),
        *pair(stage2.T.copy()),
        *pair(last),
        jnp.asarray(np.cos(twist), jnp.float32),
        jnp.asarray(np.sin(twist), jnp.float32),
    )


def split(x):
    high = x.astype(jnp.bfloat16)
    return high, (x - high.astype(jnp.float32)).astype(jnp.bfloat16)


def dot(a, b):
    return jnp.dot(a, b, preferred_element_type=jnp.float32)


def product(left, right):
    return dot(left[0], right[0]) + (dot(left[1], right[0]) + dot(left[0], right[1]))


def forward(arrays, first, second, cos_t, sin_t):
    rows, cols = cos_t.shape
    t = product(first, split(jnp.concatenate(arrays, axis=1)))
    parts = []
    for i in range(len(arrays)):
        re = t[:rows, i * cols : (i + 1) * cols]
        im = t[rows:, i * cols : (i + 1) * cols]
        parts.append(jnp.concatenate([re * cos_t + im * sin_t, im * cos_t - re * sin_t], axis=1))
    spec = product(split(jnp.concatenate(parts, axis=0)), second)
    return [
        (spec[i * rows : (i + 1) * rows, :cols], spec[i * rows : (i + 1) * rows, cols:])
        for i in range(len(arrays))
    ]


def backward(spectra, third, last, cos_t, sin_t):
    rows, cols = cos_t.shape
    prods = jnp.concatenate([jnp.concatenate(s, axis=1) for s in spectra], axis=0)
    back = product(split(prods), third)
    turns = []
    for i in range(len(spectra)):
        re, im = back[i * rows : (i + 1) * rows, :cols], back[i * rows : (i + 1) * rows, cols:]
        turns.append(
            jnp.concatenate([re * cos_t - im * sin_t, im * cos_t + re * sin_t], axis=0)
        )
    out = product(last, split(jnp.concatenate(turns, axis=1)))
    return [out[:, i * cols : (i + 1) * cols] for i in range(len(spectra))]


def read(ref, lane, group):
    if len(ref.shape) == 3:
        return ref[0, pl.ds(lane, ref.shape[1] // group, stride=group), :]
    count = ref.shape[2] // group
    return jnp.concatenate(
        [ref[b, 0, pl.ds(lane, count, stride=group), :] for b in range(ref.shape[0])], axis=0
    )


def write(ref, lane, group, value):
    if len(ref.shape) == 3:
        ref[0, pl.ds(lane, ref.shape[1] // group, stride=group), :] = value
        return
    count = ref.shape[2] // group
    for b in range(ref.shape[0]):
        ref[b, 0, pl.ds(lane, count, stride=group), :] = value[b * count : (b + 1) * count]


def kernel(group, a, b, w1h, w1l, w2h, w2l, w3h, w3l, w4h, w4l, ct, st, out):
    cos_t, sin_t = ct[...], st[...]
    first, second = (w1h[...], w1l[...]), (w2h[...], w2l[...])
    third, last = (w3h[...], w3l[...]), (w4h[...], w4l[...])
    count = 2 if group % 2 == 0 else 1

    def step(i, carry):
        lanes = [i * count + j for j in range(count)]
        xs = [read(a, lane, group) for lane in lanes] + [read(b, lane, group) for lane in lanes]
        specs = forward(xs, first, second, cos_t, sin_t)
        prods = []
        for (a_re, a_im), (b_re, b_im) in zip(specs[:count], specs[count:]):
            prods.append((a_re * b_re + a_im * b_im, a_re * b_im - a_im * b_re))
        for lane, value in zip(lanes, backward(prods, third, last, cos_t, sin_t)):
            write(out, lane, group, value)
        return carry

    lax.fori_loop(0, group // count, step, 0)


def correlate(a, b, out_shape, group, name, tabs):
    groups = b.shape[1]

    def spec(shape):
        if len(shape) == 3:
            return pl.BlockSpec((1, *shape[1:]), lambda i: (i, 0, 0))
        return pl.BlockSpec((shape[0], 1, *shape[2:]), lambda i: (0, i, 0, 0))

    rows, cols = tabs[-1].shape
    flops = 2 * 3 * groups * group * rows * cols * 3 * (2 * rows + 4 * cols)
    return pl.pallas_call(
        functools.partial(kernel, group),
        grid=(groups,),
        in_specs=[spec(a.shape), spec(b.shape)]
        + [pl.BlockSpec(t.shape, lambda i: (0, 0)) for t in tabs],
        out_specs=spec(out_shape),
        out_shape=jax.ShapeDtypeStruct(out_shape, jnp.float32),
        compiler_params=pltpu.CompilerParams(vmem_limit_bytes=56 * 1024 * 1024),
        cost_estimate=pl.CostEstimate(
            flops=flops, bytes_accessed=3 * 4 * a.size, transcendentals=0
        ),
        name=name,
    )(a, b, *tabs)


def local(signal, cotangent, first_layer, second_layer, decay_rate, skip_gain):
    parts = lax.axis_size("batch")
    place = lax.axis_index("batch")
    width_dev, local_len = signal.shape
    length = local_len * parts
    factor = 1.0 / math.sqrt(length)
    narrow = width_dev // parts
    group = min(8, narrow)
    groups = narrow // group
    rows = length // LANES
    tabs = tables(rows, LANES)

    def spread(x):
        x = x.reshape(parts, groups, group, local_len // LANES, LANES)
        x = x.transpose(0, 1, 3, 2, 4).reshape(parts, groups, -1, LANES)
        return lax.all_to_all(x, "batch", split_axis=0, concat_axis=0, tiled=True)

    def tiled(x):
        x = x.reshape(groups, group, rows, LANES).transpose(0, 2, 1, 3)
        return x.reshape(groups, rows * group, LANES)

    cot = spread(cotangent)
    positions = jnp.arange(length, dtype=jnp.int32)
    columns = lax.dynamic_slice_in_dim(second_layer, place * narrow, narrow, 1)
    rates = lax.dynamic_slice_in_dim(decay_rate, place * narrow, narrow, 0)
    gains = lax.dynamic_slice_in_dim(skip_gain, place * narrow, narrow, 0)
    embed = features(positions, length, first_layer.shape[0] // 2)
    before = jnp.dot(first_layer.T, embed, precision=exact)
    basis, slope = sincos(before)
    fraction = positions.astype(jnp.float32) / length
    window = jnp.exp(-rates[:, None] * fraction[None, :])
    shaped = window * jnp.dot(columns.T, basis, precision=precise)
    norms = jnp.sqrt(jnp.sum(shaped * shaped, axis=1, keepdims=True) + epsilon)
    filt = shaped / norms
    taps = tiled(filt + jnp.where(positions[None, :] == 0, gains[:, None], 0.0))
    cot, signal, taps, basis, slope = lax.optimization_barrier((cot, signal, taps, basis, slope))
    val = spread(signal)
    in_grad = correlate(taps, cot, cot.shape, group, "input_grad", tabs)
    val, in_grad = lax.optimization_barrier((val, in_grad))
    input_grad = lax.all_to_all(in_grad, "batch", split_axis=0, concat_axis=0, tiled=True)
    filt_grad = correlate(val, cot, taps.shape, group, "filter_grad", tabs)
    input_grad = input_grad.reshape(parts, groups, local_len // LANES, group, LANES)
    input_grad = input_grad.transpose(0, 1, 3, 2, 4).reshape(width_dev, local_len)
    filt_grad = filt_grad.reshape(groups, rows, group, LANES).transpose(0, 2, 1, 3)
    dfilt = factor * filt_grad.reshape(narrow, length)
    skip_part = (cot * val).reshape(parts, groups, local_len // LANES, group, LANES)
    skip_part = factor * jnp.sum(skip_part, axis=(0, 2, 4)).reshape(narrow)
    project = jnp.sum(filt * dfilt, axis=1, keepdims=True)
    draw = (dfilt - filt * project) / norms
    decay_part = -jnp.sum(draw * shaped * fraction[None, :], axis=1)
    dmix = draw * window
    second_part = jnp.dot(basis, dmix.T, precision=precise)
    dbasis = jnp.dot(columns, dmix, precision=precise)
    first_part = jnp.dot(embed, (slope * dbasis).T, precision=precise)
    packed = jnp.concatenate([second_part, decay_part[None], skip_part[None]], axis=0)
    packed, first_part, input_grad = lax.optimization_barrier((packed, first_part, input_grad))
    packed = lax.all_gather(packed, "batch", axis=1, tiled=True)
    first_grad = lax.psum(first_part, ("batch", "chan"))
    order = second_layer.shape[0]
    return (input_grad, first_grad, packed[:order], packed[order], packed[order + 1])


def solution(mesh):
    placed = (P("chan", "batch"), P("chan", "batch"), P(), P(None, "chan"), P("chan"), P("chan"))
    return jax.shard_map(
        local,
        mesh=mesh,
        in_specs=placed,
        out_specs=(P("chan", "batch"), P(), P(None, "chan"), P("chan"), P("chan")),
        check_vma=False,
    )
```

time: 524 us -> 371 us (0.71); the launches traced: 513 us -> 370 us
  blocking collectives: 157 us -> 68.7 us
  local copies, waits for them, and re-layouts: 44.7 us -> 8.95 us
  waiting for transfers between devices: 142 us -> 130 us
    all_gather x1, blocking collectives: 98.6 us -> 30.5 us  [local(): packed = lax.all_gather(packed, 'batch', axis=1, tiled=True)]
    unnamed x1 -> x0, blocking collectives: 20.3 us -> none
    unnamed x33 -> x24, local copies, waits for them, and re-layouts: 23.8 us -> 7.8 us
    all_to_all x3 -> x0, local copies, waits for them, and re-layouts: 14.2 us -> none  [the longest x2 9.59 us: spread(): return lax.all_to_all(x, 'batch', split_axis=0, concat_axis=1, tiled=True)]
    all_to_all x3, waiting for transfers between devices: 142 us -> 130 us  [the longest x2 110 us: spread(): return lax.all_to_all(x, 'batch', split_axis=0, concat_axis=0, tiled=True)]
    dot_general x1, matrix products: 15.5 us -> 6.31 us  [local(): dbasis = jnp.dot(columns, dmix, precision=precise)]
    pallas_call x1 -> x0, local copies, waits for them, and re-layouts: 6.63 us -> none  [correlate(): pl.pallas_call(functools.partial(kernel, count), grid=(channels // count,...]
    pallas_call x1 -> x2, Pallas kernels: 87.1 us -> 86.8 us  [correlate(): pl.pallas_call(functools.partial(kernel, group), grid=(groups,), in_specs...]
  transfers between devices with their start and end apart: 3 -> 3, of which waited for: 2 -> 3; matrix products, arithmetic and copies ran while one was open for 16% -> 16% of each run, Pallas kernels for 0% -> 23%
where the time goes in v1:
time: 371 us; the launch traced here: 370 us
  waiting for transfers between devices  130 us (35%)
  Pallas kernels  86.8 us (23%)
  blocking collectives  68.7 us (19%)
  matrix products  42.3 us (11%)
  starting transfers between devices  16.7 us (5%)
  other arithmetic  16.3 us (4%)
  local copies, waits for them, and re-layouts  8.95 us (2%)
    all_to_all x2, waiting for transfers between devices, spread(): return lax.all_to_all(x, 'batch', split_axis=0, concat_axis=0, tiled=True)  110 us
    pallas_call x2, Pallas kernels, correlate(): pl.pallas_call(functools.partial(kernel, group), grid=(groups,), in_specs...  86.8 us
    psum x1, blocking collectives, local(): first_grad = lax.psum(first_part, ('batch', 'chan'))  38.1 us
    all_gather x1, blocking collectives, local(): packed = lax.all_gather(packed, 'batch', axis=1, tiled=True)  30.5 us
    all_to_all x1, waiting for transfers between devices, local(): lax.all_to_all(in_grad, 'batch', split_axis=0, concat_axis=0, tiled=True)  19.9 us
    dot_general x1, matrix products, local(): before = jnp.dot(first_layer.T, embed, precision=exact)  19.3 us
    all_to_all x2, starting transfers between devices, spread(): return lax.all_to_all(x, 'batch', split_axis=0, concat_axis=0, tiled=True)  12.2 us
    dot_general x1, matrix products, local(): second_part = jnp.dot(basis, dmix.T, precision=precise)  8.57 us
  transfers between devices with their start and end apart: 3, of which 3 were waited for; matrix products, arithmetic and copies ran while one was open for 16% of the time, Pallas kernels for 23%

profile of v1, /device:TPU:0, one launch (start us, length us, event | category | flops | bytes accessed | tf_op | source)
XLA Modules:
  0.0 370.3 jit_solution(5105373715380031526)
XLA Ops:
  0.7 7.4 %all-to-all-start = ((f32[8,4,256,128]{3,2,1,0:T(8,128)}), f32[8,4,256,128]{3,2,1,0:T(8,128)}, u32[]{:S(2)}, u32[]{:S(2)}) async-start(f32[8,4,256,128]{3,2,1,0:T(8,128)} %bitcast.42), calls=%async_computation | async-start | bytes 8388608 | tf_op jit(solution)/shard_map/all_to_all | solution.py:194
  8.2 0.1 dynamic-slice_negate_fusion
  8.2 0.1 dynamic_slice.11
  8.3 3.6 negate_select_fusion.3
  11.9 0.1 convert_multiply_fusion
  12.1 19.3 %negate_select_fusion = (f32[64,32768]{1,0:T(8,128)}, f32[64,32768]{1,0:T(8,128)S(1)}) fusion(f32[33,64]{1,0:T(8,128)S(1)} %copy-done.8, f32[16,32768]{1,0:T(8,128)S(1)} %get-tuple-element.42, f32[16,32768]{1,0:T(8,128)S(1)} %get-tuple-element.41, f32[1,32768]{1,0:T(1,128)S(1)} %convert_multiply_fusion), kind=kOutput, calls=%fused_computation.3 | convolution fusion | flops 914423808 | bytes 21111040 | tf_op jit(solution)/shard_map/dot_general | solution.py:206
  31.4 4.4 %multiply_reduce_fusion.2 = (f32[32]{0:T(128)S(1)}, f32[32,32768]{1,0:T(8,128)S(1)}) fusion(f32[64,32768]{1,0:T(8,128)S(1)} %get-tuple-element.15, f32[64,256]{1,0:T(8,128)S(1)} %copy-done, s32[]{:T(128)S(6)} %select_n.44, f32[32768]{0:T(1024)S(1)} %convert_multiply_fusion.1, f32[32]{0:T(128)S(1)} %dynamic-slice_negate_fusion), kind=kOutput, calls=%fused_computation.33 | convolution fusion | flops 406847456 | bytes 12747396 | tf_op jit(solution)/shard_map/dot_general | solution.py:210
  35.9 2.0 copy-done.1
  37.9 2.6 add_bitcast_fusion.a
  40.5 60.9 %all-to-all-done.b = f32[8,4,256,128]{3,2,1,0:T(8,128)} async-done(((f32[8,4,256,128]{3,2,1,0:T(8,128)}), f32[8,4,256,128]{3,2,1,0:T(8,128)}, u32[]{:S(2)}, u32[]{:S(2)}) %all-to-all-start) | async-done | bytes 4194336 | tf_op jit(solution)/shard_map/all_to_all | solution.py:194
  101.4 4.8 %all-to-all-start.1 = ((f32[8,4,256,128]{3,2,1,0:T(8,128)}), f32[8,4,256,128]{3,2,1,0:T(8,128)}, u32[]{:S(2)}, u32[]{:S(2)}) async-start(f32[8,4,256,128]{3,2,1,0:T(8,128)} %bitcast.43), calls=%async_computation.1 | async-start | bytes 8388608 | tf_op jit(solution)/shard_map/all_to_all | solution.py:194
  106.1 43.4 %input_grad.1 = f32[8,4,256,128]{3,2,1,0:T(8,128)} custom-call(f32[4,2048,128]{2,1,0:T(8,128)} %add_bitcast_fusion.a, f32[8,4,256,128]{3,2,1,0:T(8,128)} %all-to-all-done.b, bf16[512,256]{1,0:T(8,128)(2,1)} %constant.31.clone.w1h, bf16[512,256]{1,0:T(8,128)(2,1)} %constant.32.clone.w1l, bf16[256,256]{1,0:T(8,128)(2,1)} %constant.33.clone.w2h, ...), custom_call_target="tpu_custom_call" | custom-call | flops 19327352832 | bytes 12582912 | tf_op jit(solution)/shard_map/input_grad/pallas_call | solution.py:164
  149.5 49.0 %all-to-all-done.1.a = f32[8,4,256,128]{3,2,1,0:T(8,128)} async-done(((f32[8,4,256,128]{3,2,1,0:T(8,128)}), f32[8,4,256,128]{3,2,1,0:T(8,128)}, u32[]{:S(2)}, u32[]{:S(2)}) %all-to-all-start.1) | async-done | bytes 4194336 | tf_op jit(solution)/shard_map/all_to_all | solution.py:194
  198.5 4.6 %all-to-all-start.2 = ((f32[8,4,256,128]{3,2,1,0:T(8,128)}), f32[8,4,256,128]{3,2,1,0:T(8,128)}, u32[]{:S(2)}, u32[]{:S(2)}) async-start(f32[8,4,256,128]{3,2,1,0:T(8,128)} %input_grad.1), calls=%async_computation.2 | async-start | bytes 8388608 | tf_op jit(solution)/shard_map/all_to_all | solution.py:218
  203.1 43.5 %filter_grad.1 = f32[4,2048,128]{2,1,0:T(8,128)} custom-call(f32[8,4,256,128]{3,2,1,0:T(8,128)} %all-to-all-done.1.a, f32[8,4,256,128]{3,2,1,0:T(8,128)} %all-to-all-done.b, bf16[512,256]{1,0:T(8,128)(2,1)} %constant.31.clone.w1h, bf16[512,256]{1,0:T(8,128)(2,1)} %constant.32.clone.w1l, bf16[256,256]{1,0:T(8,128)(2,1)} %constant.33.clone.w2h, ...), custom_call_target="tpu_custom_call" | custom-call | flops 19327352832 | bytes 12582912 | tf_op jit(solution)/shard_map/filter_grad/pallas_call | solution.py:164
  246.6 3.1 fusion.9
  249.6 0.4 copy-done.5
  250.0 2.8 multiply_reduce_fusion.1
  252.8 0.1 copy.24
  252.9 3.9 %multiply_reduce_fusion = f32[4,256]{1,0:T(4,128)S(1)} fusion(f32[8,4,256,128]{3,2,1,0:T(8,128)} %all-to-all-done.b, f32[8,4,256,128]{3,2,1,0:T(8,128)} %all-to-all-done.1.a), kind=kLoop, calls=%fused_computation.30 | loop fusion | flops 2096128 | bytes 8392704 | tf_op jit(solution)/shard_map/reduce_sum | solution.py:225
  256.8 0.1 reduce_sum.47
  256.9 0.1 mul.336
  257.0 8.6 %fusion.14 = f32[64,32]{0,1:T(8,128)S(1)} fusion(f32[64,32768]{1,0:T(8,128)} %copy-done.4, f32[32,32768]{1,0:T(8,128)} %get-tuple-element.38, f32[32768]{0:T(1024)S(1)} %convert_multiply_fusion.1, f32[32]{0:T(128)S(1)} %dynamic-slice_negate_fusion), kind=kOutput, calls=%fused_computation.37 | convolution fusion | flops 404750336 | bytes 12722304 | tf_op jit(solution)/shard_map/dot_general | solution.py:230
  265.6 0.1 pad_maximum_fusion.3
  265.7 6.3 %convolution_multiply_fusion = f32[64,32768]{1,0:T(8,128)S(1)} fusion(f32[64,32768]{1,0:T(8,128)} %get-tuple-element.20, f32[32,32768]{1,0:T(8,128)S(1)} %copy-done.3, f32[32768]{0:T(1024)S(1)} %convert_multiply_fusion.1, f32[32]{0:T(128)S(1)} %dynamic-slice_negate_fusion, f32[64,256]{1,0:T(8,128)S(1)} %copy-done, s32[]{:T(128)S(6)} %select_n.44), kind=kOutput, calls=%fused_computation | convolution fusion | flops 406847488 | bytes 21135876 | tf_op jit(solution)/shard_map/dot_general | solution.py:231
  272.0 3.7 fusion.12
  275.7 19.9 %all-to-all-done.2 = f32[8,4,256,128]{3,2,1,0:T(8,128)} async-done(((f32[8,4,256,128]{3,2,1,0:T(8,128)}), f32[8,4,256,128]{3,2,1,0:T(8,128)}, u32[]{:S(2)}, u32[]{:S(2)}) %all-to-all-start.2) | async-done | bytes 4194336 | tf_op jit(solution)/shard_map/all_to_all | solution.py:218
  295.5 38.1 %psum.7 = f32[33,64]{1,0:T(8,128)} all-reduce(f32[33,64]{1,0:T(8,128)S(1)} %fusion.12), channel_id=1, replica_groups=mesh['batch'=8,'chan'=4] {'batch','chan'}, use_global_device_ids=true, to_apply=%region_5.6 | all-reduce | flops 2112 | bytes 16896 | tf_op jit(solution)/shard_map/psum | solution.py:236
  333.7 30.5 %all_gather.3 = f32[66,256]{0,1:T(8,128)S(1)} all-gather(f32[66,32]{0,1:T(8,128)S(1)} %pad_maximum_fusion.3), channel_id=1, replica_groups=mesh['batch'=8,'chan'=4] {'batch'}, dimensions={1}, use_global_device_ids=true | all-gather | bytes 76032 | tf_op jit(solution)/shard_map/all_gather | solution.py:235
  364.2 0.8 slice_reduce_fusion
  365.0 0.7 copy.26
  365.7 4.7 %copy.28 = f32[256,4096]{1,0:T(8,128)} copy(f32[256,4096]{1,0:T(8,128)} %bitcast.18) | data formatting | bytes 8388608
  (27 shorter events, 0.1 us)
Async XLA Ops:
  0.6 30.8 %copy-start = (f32[64,256]{1,0:T(8,128)S(1)}, f32[64,256]{1,0:T(8,128)}, u32[]{:S(2)}) copy-start(f32[64,256]{1,0:T(8,128)} %param.19) | copy-start | bytes 196612
  0.6 7.5 %copy-start.9 = (f32[256]{0:T(256)S(1)}, f32[256]{0:T(256)}, u32[]{:S(2)}) copy-start(f32[256]{0:T(256)} %param.20) | copy-start | bytes 3076
  0.7 7.6 %copy-start.10 = (f32[256]{0:T(256)S(1)}, f32[256]{0:T(256)}, u32[]{:S(2)}) copy-start(f32[256]{0:T(256)} %param.21) | copy-start | bytes 3076
  0.7 100.7 %all-to-all-start = ((f32[8,4,256,128]{3,2,1,0:T(8,128)}), f32[8,4,256,128]{3,2,1,0:T(8,128)}, u32[]{:S(2)}, u32[]{:S(2)}) async-start(f32[8,4,256,128]{3,2,1,0:T(8,128)} %bitcast.42), calls=%async_computation | async-start | bytes 8388608 | tf_op jit(solution)/shard_map/all_to_all | solution.py:194
  8.1 4.0 %copy-start.8 = (f32[33,64]{1,0:T(8,128)S(1)}, f32[33,64]{1,0:T(8,128)}, u32[]{:S(2)}) copy-start(f32[33,64]{1,0:T(8,128)} %param.18) | copy-start | bytes 25348
  11.9 19.5 %copy-start.6 = (f32[16,32768]{1,0:T(8,128)}, f32[16,32768]{1,0:T(8,128)S(1)}, u32[]{:S(2)}) copy-start(f32[16,32768]{1,0:T(8,128)S(1)} %get-tuple-element.42) | copy-start | bytes 6291460
  31.4 4.4 %copy-start.4 = (f32[64,32768]{1,0:T(8,128)}, f32[64,32768]{1,0:T(8,128)S(1)}, u32[]{:S(2)}) copy-start(f32[64,32768]{1,0:T(8,128)S(1)} %get-tuple-element.15) | copy-start | bytes 25165828
  35.8 2.0 copy-start.1
  101.4 97.1 %all-to-all-start.1 = ((f32[8,4,256,128]{3,2,1,0:T(8,128)}), f32[8,4,256,128]{3,2,1,0:T(8,128)}, u32[]{:S(2)}, u32[]{:S(2)}) async-start(f32[8,4,256,128]{3,2,1,0:T(8,128)} %bitcast.43), calls=%async_computation.1 | async-start | bytes 8388608 | tf_op jit(solution)/shard_map/all_to_all | solution.py:194
  198.5 97.0 %all-to-all-start.2 = ((f32[8,4,256,128]{3,2,1,0:T(8,128)}), f32[8,4,256,128]{3,2,1,0:T(8,128)}, u32[]{:S(2)}, u32[]{:S(2)}) async-start(f32[8,4,256,128]{3,2,1,0:T(8,128)} %input_grad.1), calls=%async_computation.2 | async-start | bytes 8388608 | tf_op jit(solution)/shard_map/all_to_all | solution.py:218
  203.1 43.5 %copy-start.2 = (f32[32,32768]{1,0:T(8,128)S(1)}, f32[32,32768]{1,0:T(8,128)}, u32[]{:S(2)}) copy-start(f32[32,32768]{1,0:T(8,128)} %copy-done.1) | copy-start | bytes 12582916
  246.6 3.5 copy-start.5
  257.0 8.7 %copy-start.3 = (f32[32,32768]{1,0:T(8,128)S(1)}, f32[32,32768]{1,0:T(8,128)}, u32[]{:S(2)}) copy-start(f32[32,32768]{1,0:T(8,128)} %get-tuple-element.38) | copy-start | bytes 12582916
  265.7 6.3 %copy-start.7 = (f32[16,32768]{1,0:T(8,128)S(1)}, f32[16,32768]{1,0:T(8,128)}, u32[]{:S(2)}) copy-start(f32[16,32768]{1,0:T(8,128)} %copy-done.6) | copy-start | bytes 6291460

commit v2 on v1

--- a/solution.py
+++ b/solution.py
@@ -174,6 +174,92 @@
         ),
         name=name,
     )(a, b, *tabs)
+
+
+MESH = pl.DeviceIdType.MESH
+
+
+def share_kernel(parts, chans, mine, shared, total, slots, partial, sums, sends, arrivals, sends2, arrivals2):
+    me, my_chan = lax.axis_index("batch"), lax.axis_index("chan")
+    barrier = pltpu.get_barrier_semaphore()
+    for k in range(1, parts):
+        peer = lax.rem(me + k, parts)
+        pl.semaphore_signal(barrier, inc=1, device_id=(peer, my_chan), device_id_type=MESH)
+    for k in range(1, chans):
+        peer = lax.rem(my_chan + k, chans)
+        pl.semaphore_signal(barrier, inc=1, device_id=(me, peer), device_id_type=MESH)
+    pl.semaphore_wait(barrier, parts + chans - 2)
+    copies = []
+    for k in range(1, parts):
+        copies.append(
+            pltpu.make_async_remote_copy(
+                src_ref=mine,
+                dst_ref=slots.at[k],
+                send_sem=sends.at[k],
+                recv_sem=arrivals.at[k],
+                device_id=(lax.rem(me + k, parts), my_chan),
+                device_id_type=MESH,
+            )
+        )
+        copies[-1].start()
+    slots[0] = mine[...]
+    for copy in copies:
+        copy.wait_recv()
+    acc = jnp.zeros(mine.shape, jnp.float32)
+    for b in range(parts):
+        block = slots[lax.rem(me + parts - b, parts)]
+        shared[b] = block
+        acc = acc + block
+    partial[...] = acc
+    for copy in copies:
+        copy.wait_send()
+    copies = []
+    for k in range(1, chans):
+        copies.append(
+            pltpu.make_async_remote_copy(
+                src_ref=partial,
+                dst_ref=sums.at[k],
+                send_sem=sends2.at[k],
+                recv_sem=arrivals2.at[k],
+                device_id=(me, lax.rem(my_chan + k, chans)),
+                device_id_type=MESH,
+            )
+        )
+        copies[-1].start()
+    sums[0] = acc
+    for copy in copies:
+        copy.wait_recv()
+    acc = jnp.zeros_like(acc)
+    for c in range(chans):
+        acc = acc + sums[lax.rem(my_chan + chans - c, chans)]
+    total[...] = acc
+    for copy in copies:
+        copy.wait_send()
+
+
+def share(block, parts, chans):
+    vmem = pl.BlockSpec(memory_space=pltpu.VMEM)
+    dma = pltpu.SemaphoreType.DMA
+    return pl.pallas_call(
+        functools.partial(share_kernel, parts, chans),
+        in_specs=[vmem],
+        out_specs=[vmem, vmem],
+        out_shape=[
+            jax.ShapeDtypeStruct((parts, *block.shape), jnp.float32),
+            jax.ShapeDtypeStruct(block.shape, jnp.float32),
+        ],
+        scratch_shapes=[
+            pltpu.VMEM((parts, *block.shape), jnp.float32),
+            pltpu.VMEM(block.shape, jnp.float32),
+            pltpu.VMEM((chans, *block.shape), jnp.float32),
+            dma((parts,)),
+            dma((parts,)),
+            dma((chans,)),
+            dma((chans,)),
+        ],
+        compiler_params=pltpu.CompilerParams(collective_id=0, has_side_effects=True),
+        name="share",
+    )(block)
 
 
 def local(signal, cotangent, first_layer, second_layer, decay_rate, skip_gain):
@@ -227,15 +313,23 @@
     draw = (dfilt - filt * project) / norms
     decay_part = -jnp.sum(draw * shaped * fraction[None, :], axis=1)
     dmix = draw * window
-    second_part = jnp.dot(basis, dmix.T, precision=precise)
+    second_part = jnp.dot(dmix, basis.T, precision=precise)
     dbasis = jnp.dot(columns, dmix, precision=precise)
     first_part = jnp.dot(embed, (slope * dbasis).T, precision=precise)
-    packed = jnp.concatenate([second_part, decay_part[None], skip_part[None]], axis=0)
-    packed, first_part, input_grad = lax.optimization_barrier((packed, first_part, input_grad))
-    packed = lax.all_gather(packed, "batch", axis=1, tiled=True)
-    first_grad = lax.psum(first_part, ("batch", "chan"))
-    order = second_layer.shape[0]
-    return (input_grad, first_grad, packed[:order], packed[order], packed[order + 1])
+    bands, order = first_layer.shape
+    left = jnp.concatenate([decay_part, skip_part])
+    left = jnp.concatenate([first_part, jnp.pad(left, (0, order - 2 * narrow))[None]], axis=0)
+    high = -(-max(bands + 1, narrow) // 8) * 8
+    left = jnp.pad(left, ((0, high - bands - 1), (0, 0)))
+    right = jnp.pad(second_part, ((0, high - narrow), (0, 0)))
+    block = jnp.concatenate([left, right], axis=1)
+    block, input_grad = lax.optimization_barrier((block, input_grad))
+    shared, total = share(block, parts, lax.axis_size("chan"))
+    first_grad = total[:bands, :order]
+    second_grad = shared[:, :narrow, order:].reshape(width_dev, order).T
+    decay_grad = shared[:, bands, :narrow].reshape(width_dev)
+    skip_grad = shared[:, bands, narrow : 2 * narrow].reshape(width_dev)
+    return (input_grad, first_grad, second_grad, decay_grad, skip_grad)
 
 
 def solution(mesh):

time: 371 us -> 317 us (0.85)
  blocking collectives: 68.7 us -> 0 us
  Pallas kernels: 86.8 us -> 98.3 us
    psum x1 -> x0, blocking collectives: 38.1 us -> none  [local(): first_grad = lax.psum(first_part, ('batch', 'chan'))]
    all_gather x1 -> x0, blocking collectives: 30.5 us -> none  [local(): packed = lax.all_gather(packed, 'batch', axis=1, tiled=True)]
    pallas_call x0 -> x1, Pallas kernels: none -> 11.5 us  [share(): pl.pallas_call(functools.partial(share_kernel, parts, chans), in_specs=[v...]
    dot_general x1, matrix products: 8.57 us -> 3.73 us  [local(): second_part = jnp.dot(dmix, basis.T, precision=precise)]
    unnamed x24 -> x28, local copies, waits for them, and re-layouts: 7.8 us -> 7.72 us
  transfers between devices with their start and end apart: 3 -> 3, of which waited for: 3 -> 3; matrix products, arithmetic and copies ran while one was open for 16% -> 18% of each run, Pallas kernels for 23% -> 27%
where the time goes in v2:
time: 317 us; the launch traced here: 316 us
  waiting for transfers between devices  131 us (41%)
  Pallas kernels  98.3 us (31%)
  matrix products  41 us (13%)
  other arithmetic  17 us (5%)
  starting transfers between devices  16.7 us (5%)
  local copies, waits for them, and re-layouts  11.9 us (4%)
    all_to_all x2, waiting for transfers between devices, spread(): return lax.all_to_all(x, 'batch', split_axis=0, concat_axis=0, tiled=True)  110 us
    pallas_call x2, Pallas kernels, correlate(): pl.pallas_call(functools.partial(kernel, group), grid=(groups,), in_specs...  86.8 us
    all_to_all x1, waiting for transfers between devices, local(): lax.all_to_all(in_grad, 'batch', split_axis=0, concat_axis=0, tiled=True)  20.5 us
    dot_general x1, matrix products, local(): before = jnp.dot(first_layer.T, embed, precision=exact)  19.3 us
    all_to_all x2, starting transfers between devices, spread(): return lax.all_to_all(x, 'batch', split_axis=0, concat_axis=0, tiled=True)  12.2 us
    pallas_call x1, Pallas kernels, share(): pl.pallas_call(functools.partial(share_kernel, parts, chans), in_specs=[v...  11.5 us
    dot_general x1, matrix products, local(): dbasis = jnp.dot(columns, dmix, precision=precise)  8.09 us
    unnamed x28, local copies, waits for them, and re-layouts  7.72 us
  transfers between devices with their start and end apart: 3, of which 3 were waited for; matrix products, arithmetic and copies ran while one was open for 18% of the time, Pallas kernels for 27%

profile of v2, /device:TPU:0, one launch (start us, length us, event | category | flops | bytes accessed | tf_op | source)
XLA Modules:
  0.0 316.2 jit_solution(15879530722379507112)
XLA Ops:
  0.7 7.4 %all-to-all-start = ((f32[8,4,256,128]{3,2,1,0:T(8,128)}), f32[8,4,256,128]{3,2,1,0:T(8,128)}, u32[]{:S(2)}, u32[]{:S(2)}) async-start(f32[8,4,256,128]{3,2,1,0:T(8,128)} %bitcast.46), calls=%async_computation | async-start | bytes 8388608 | tf_op jit(solution)/shard_map/all_to_all | solution.py:280
  8.3 3.6 %negate_select_fusion.3 = (f32[16,32768]{1,0:T(8,128)S(1)}, f32[16,32768]{1,0:T(8,128)S(1)}) fusion(s32[16]{0:T(128)S(1)} %iota_add_fusion), kind=kLoop, calls=%fused_computation.39 | loop fusion | flops 27787264 | bytes 4194368 | tf_op jit(solution)/shard_map/jit(_where)/select_n | solution.py:34
  11.9 0.1 convert_multiply_fusion.1
  12.1 19.3 %negate_select_fusion = (f32[64,32768]{1,0:T(8,128)}, f32[64,32768]{1,0:T(8,128)S(1)}) fusion(f32[33,64]{1,0:T(8,128)S(1)} %copy-done.8, f32[16,32768]{1,0:T(8,128)S(1)} %get-tuple-element.34, f32[16,32768]{1,0:T(8,128)S(1)} %get-tuple-element.33, f32[1,32768]{1,0:T(1,128)S(1)} %convert_multiply_fusion.1), kind=kOutput, calls=%fused_computation.3 | convolution fusion | flops 914423808 | bytes 21111040 | tf_op jit(solution)/shard_map/dot_general | solution.py:292
  31.4 4.4 %multiply_reduce_fusion.2 = (f32[32]{0:T(128)S(1)}, f32[32,32768]{1,0:T(8,128)S(1)}) fusion(f32[64,32768]{1,0:T(8,128)S(1)} %get-tuple-element.21, f32[64,256]{1,0:T(8,128)S(1)} %copy-done, s32[]{:T(128)S(6)} %select_n.49, f32[32768]{0:T(1024)S(1)} %convert_multiply_fusion, f32[32]{0:T(128)S(1)} %dynamic-slice_negate_fusion), kind=kOutput, calls=%fused_computation.33 | convolution fusion | flops 406847456 | bytes 12747396 | tf_op jit(solution)/shard_map/dot_general | solution.py:296
  35.9 2.0 copy-done.1
  37.9 2.6 add_bitcast_fusion.a
  40.4 60.9 %all-to-all-done.b = f32[8,4,256,128]{3,2,1,0:T(8,128)} async-done(((f32[8,4,256,128]{3,2,1,0:T(8,128)}), f32[8,4,256,128]{3,2,1,0:T(8,128)}, u32[]{:S(2)}, u32[]{:S(2)}) %all-to-all-start) | async-done | bytes 4194336 | tf_op jit(solution)/shard_map/all_to_all | solution.py:280
  101.4 4.8 %all-to-all-start.1 = ((f32[8,4,256,128]{3,2,1,0:T(8,128)}), f32[8,4,256,128]{3,2,1,0:T(8,128)}, u32[]{:S(2)}, u32[]{:S(2)}) async-start(f32[8,4,256,128]{3,2,1,0:T(8,128)} %bitcast.47), calls=%async_computation.1 | async-start | bytes 8388608 | tf_op jit(solution)/shard_map/all_to_all | solution.py:280
  106.1 43.3 %input_grad.1 = f32[8,4,256,128]{3,2,1,0:T(8,128)} custom-call(f32[4,2048,128]{2,1,0:T(8,128)} %add_bitcast_fusion.a, f32[8,4,256,128]{3,2,1,0:T(8,128)} %all-to-all-done.b, bf16[512,256]{1,0:T(8,128)(2,1)} %constant.32.clone.w1h, bf16[512,256]{1,0:T(8,128)(2,1)} %constant.33.clone.w1l, bf16[256,256]{1,0:T(8,128)(2,1)} %constant.34.clone.w2h, ...), custom_call_target="tpu_custom_call" | custom-call | flops 19327352832 | bytes 12582912 | tf_op jit(solution)/shard_map/input_grad/pallas_call | solution.py:164
  149.5 49.1 %all-to-all-done.1.a = f32[8,4,256,128]{3,2,1,0:T(8,128)} async-done(((f32[8,4,256,128]{3,2,1,0:T(8,128)}), f32[8,4,256,128]{3,2,1,0:T(8,128)}, u32[]{:S(2)}, u32[]{:S(2)}) %all-to-all-start.1) | async-done | bytes 4194336 | tf_op jit(solution)/shard_map/all_to_all | solution.py:280
  198.5 4.6 %all-to-all-start.2 = ((f32[8,4,256,128]{3,2,1,0:T(8,128)}), f32[8,4,256,128]{3,2,1,0:T(8,128)}, u32[]{:S(2)}, u32[]{:S(2)}) async-start(f32[8,4,256,128]{3,2,1,0:T(8,128)} %input_grad.1), calls=%async_computation.2 | async-start | bytes 8388608 | tf_op jit(solution)/shard_map/all_to_all | solution.py:304
  203.1 43.5 %filter_grad.1 = f32[4,2048,128]{2,1,0:T(8,128)} custom-call(f32[8,4,256,128]{3,2,1,0:T(8,128)} %all-to-all-done.1.a, f32[8,4,256,128]{3,2,1,0:T(8,128)} %all-to-all-done.b, bf16[512,256]{1,0:T(8,128)(2,1)} %constant.32.clone.w1h, bf16[512,256]{1,0:T(8,128)(2,1)} %constant.33.clone.w1l, bf16[256,256]{1,0:T(8,128)(2,1)} %constant.34.clone.w2h, ...), custom_call_target="tpu_custom_call" | custom-call | flops 19327352832 | bytes 12582912 | tf_op jit(solution)/shard_map/filter_grad/pallas_call | solution.py:164
  246.6 3.1 fusion.9
  249.6 0.4 copy-done.5
  250.0 2.8 multiply_reduce_fusion.1
  252.8 3.9 %multiply_reduce_fusion = f32[4,256]{1,0:T(4,128)S(1)} fusion(f32[8,4,256,128]{3,2,1,0:T(8,128)} %all-to-all-done.b, f32[8,4,256,128]{3,2,1,0:T(8,128)} %all-to-all-done.1.a), kind=kLoop, calls=%fused_computation.30 | loop fusion | flops 2096128 | bytes 8392704 | tf_op jit(solution)/shard_map/reduce_sum | solution.py:311
  256.7 0.1 reduce_sum.47
  256.8 0.1 mul.328
  257.0 8.1 %convolution_multiply_fusion = f32[64,32768]{1,0:T(8,128)S(1)} fusion(f32[64,32768]{1,0:T(8,128)} %get-tuple-element.16, f32[32,32768]{1,0:T(8,128)} %get-tuple-element.30, f32[32768]{0:T(1024)S(1)} %convert_multiply_fusion, f32[32]{0:T(128)S(1)} %dynamic-slice_negate_fusion, f32[64,256]{1,0:T(8,128)S(1)} %copy-done, s32[]{:T(128)S(6)} %select_n.49), kind=kOutput, calls=%fused_computation | convolution fusion | flops 406847488 | bytes 21135876 | tf_op jit(solution)/shard_map/dot_general | solution.py:317
  265.1 5.4 %fusion.12 = f32[33,64]{1,0:T(8,128)S(1)} fusion(f32[64,32768]{1,0:T(8,128)S(1)} %convolution_multiply_fusion, f32[16,32768]{1,0:T(8,128)} %copy-done.6, f32[16,32768]{1,0:T(8,128)S(1)} %get-tuple-element.33, f32[1,32768]{1,0:T(1,128)S(1)} %convert_multiply_fusion.1), kind=kOutput, calls=%fused_computation.36 | convolution fusion | flops 417398784 | bytes 12722432 | tf_op jit(solution)/shard_map/dot_general | solution.py:318
  270.6 3.7 %fusion.13 = f32[32,64]{1,0:T(8,128)S(1)} fusion(f32[64,32768]{1,0:T(8,128)S(1)} %bitcast.45, f32[32,32768]{1,0:T(8,128)S(1)} %copy-done.3, f32[32768]{0:T(1024)S(1)} %convert_multiply_fusion, f32[32]{0:T(128)S(1)} %dynamic-slice_negate_fusion), kind=kOutput, calls=%fused_computation.37 | convolution fusion | flops 404750336 | bytes 12722304 | tf_op jit(solution)/shard_map/dot_general | solution.py:316
  274.3 0.7 select_maximum_fusion.mine
  275.0 20.5 %all-to-all-done.2 = f32[8,4,256,128]{3,2,1,0:T(8,128)} async-done(((f32[8,4,256,128]{3,2,1,0:T(8,128)}), f32[8,4,256,128]{3,2,1,0:T(8,128)}, u32[]{:S(2)}, u32[]{:S(2)}) %all-to-all-start.2) | async-done | bytes 4194336 | tf_op jit(solution)/shard_map/all_to_all | solution.py:304
  295.5 11.5 %share.1 = (f32[8,40,128]{2,1,0:T(8,128)}, f32[40,128]{1,0:T(8,128)}) custom-call(f32[40,128]{1,0:T(8,128)} %select_maximum_fusion.mine), custom_call_target="tpu_custom_call" | custom-call | tf_op jit(solution)/shard_map/share/pallas_call | solution.py:243
  307.0 0.9 slice_reduce_fusion
  308.0 1.0 slice.13
  309.0 0.7 copy.22
  309.7 0.6 reshape_squeeze.7
  310.3 0.6 reshape_squeeze.6
  311.0 4.7 %copy.25 = f32[256,4096]{1,0:T(8,128)} copy(f32[256,4096]{1,0:T(8,128)} %bitcast.18) | data formatting | bytes 8388608
  315.6 0.6 copy.26
  (36 shorter events, 0.4 us)
Async XLA Ops:
  0.6 30.7 %copy-start = (f32[64,256]{1,0:T(8,128)S(1)}, f32[64,256]{1,0:T(8,128)}, u32[]{:S(2)}) copy-start(f32[64,256]{1,0:T(8,128)} %param.19) | copy-start | bytes 196612
  0.6 7.5 %copy-start.9 = (f32[256]{0:T(256)S(1)}, f32[256]{0:T(256)}, u32[]{:S(2)}) copy-start(f32[256]{0:T(256)} %param.20) | copy-start | bytes 3076
  0.7 7.6 %copy-start.10 = (f32[256]{0:T(256)S(1)}, f32[256]{0:T(256)}, u32[]{:S(2)}) copy-start(f32[256]{0:T(256)} %param.21) | copy-start | bytes 3076
  0.7 100.7 %all-to-all-start = ((f32[8,4,256,128]{3,2,1,0:T(8,128)}), f32[8,4,256,128]{3,2,1,0:T(8,128)}, u32[]{:S(2)}, u32[]{:S(2)}) async-start(f32[8,4,256,128]{3,2,1,0:T(8,128)} %bitcast.46), calls=%async_computation | async-start | bytes 8388608 | tf_op jit(solution)/shard_map/all_to_all | solution.py:280
  8.1 4.0 %copy-start.8 = (f32[33,64]{1,0:T(8,128)S(1)}, f32[33,64]{1,0:T(8,128)}, u32[]{:S(2)}) copy-start(f32[33,64]{1,0:T(8,128)} %param.18) | copy-start | bytes 25348
  11.9 19.4 %copy-start.6 = (f32[16,32768]{1,0:T(8,128)}, f32[16,32768]{1,0:T(8,128)S(1)}, u32[]{:S(2)}) copy-start(f32[16,32768]{1,0:T(8,128)S(1)} %get-tuple-element.34) | copy-start | bytes 6291460
  31.4 4.4 %copy-start.4 = (f32[64,32768]{1,0:T(8,128)}, f32[64,32768]{1,0:T(8,128)S(1)}, u32[]{:S(2)}) copy-start(f32[64,32768]{1,0:T(8,128)S(1)} %get-tuple-element.21) | copy-start | bytes 25165828
  35.8 2.0 copy-start.1
  101.4 97.1 %all-to-all-start.1 = ((f32[8,4,256,128]{3,2,1,0:T(8,128)}), f32[8,4,256,128]{3,2,1,0:T(8,128)}, u32[]{:S(2)}, u32[]{:S(2)}) async-start(f32[8,4,256,128]{3,2,1,0:T(8,128)} %bitcast.47), calls=%async_computation.1 | async-start | bytes 8388608 | tf_op jit(solution)/shard_map/all_to_all | solution.py:280
  198.5 97.0 %all-to-all-start.2 = ((f32[8,4,256,128]{3,2,1,0:T(8,128)}), f32[8,4,256,128]{3,2,1,0:T(8,128)}, u32[]{:S(2)}, u32[]{:S(2)}) async-start(f32[8,4,256,128]{3,2,1,0:T(8,128)} %input_grad.1), calls=%async_computation.2 | async-start | bytes 8388608 | tf_op jit(solution)/shard_map/all_to_all | solution.py:304
  203.1 43.5 %copy-start.2 = (f32[32,32768]{1,0:T(8,128)S(1)}, f32[32,32768]{1,0:T(8,128)}, u32[]{:S(2)}) copy-start(f32[32,32768]{1,0:T(8,128)} %copy-done.1) | copy-start | bytes 12582916
  246.6 3.5 %copy-start.5 = (f32[4,2048,128]{2,1,0:T(8,128)S(1)}, f32[4,2048,128]{2,1,0:T(8,128)}, u32[]{:S(2)}) copy-start(f32[4,2048,128]{2,1,0:T(8,128)} %filter_grad.1) | copy-start | bytes 12582916
  257.0 13.5 %slice-start = ((s8[8388608]{0:T(1024)(128)(4,1)}), s8[4194304]{0:T(1024)(128)(4,1)S(1)}, s32[]{:S(2)}) async-start(s8[8388608]{0:T(1024)(128)(4,1)} %bitcast.44), calls=%async_computation.3 | async-start | bytes 8388608
  257.0 13.6 %slice-start.1 = ((s8[8388608]{0:T(1024)(128)(4,1)}), s8[4194304]{0:T(1024)(128)(4,1)S(1)}, s32[]{:S(2)}) async-start(s8[8388608]{0:T(1024)(128)(4,1)} %bitcast.44), calls=%async_computation.4 | async-start | bytes 8388608
  265.1 5.5 %copy-start.3 = (f32[32,32768]{1,0:T(8,128)S(1)}, f32[32,32768]{1,0:T(8,128)}, u32[]{:S(2)}) copy-start(f32[32,32768]{1,0:T(8,128)} %get-tuple-element.30) | copy-start | bytes 12582916
  311.0 4.7 %copy-start.7 = (f32[40,128]{1,0:T(8,128)S(1)}, f32[40,128]{1,0:T(8,128)}, u32[]{:S(2)}) copy-start(f32[40,128]{1,0:T(8,128)} %get-tuple-element.25) | copy-start | bytes 61444

commit v3 on v2

--- a/solution.py
+++ b/solution.py
@@ -33,16 +33,6 @@
     sin_value = jnp.where(quadrant >= 2, -sin_value, sin_value)
     cos_value = jnp.where((quadrant == 1) | (quadrant == 2), -cos_value, cos_value)
     return sin_value, cos_value
-
-
-def features(positions, length, band_count):
-    band_index = jnp.arange(1, band_count + 1, dtype=jnp.int32)
-    phase = (band_index[:, None] * positions[None, :] % length).astype(jnp.float32) * (
-        2.0 * math.pi / length
-    )
-    linear = positions.astype(jnp.float32)[None, :] / length
-    sines, cosines = sincos(phase)
-    return jnp.concatenate([linear, cosines, sines], axis=0)
 
 
 def pair(matrix):
@@ -113,67 +103,22 @@
     return [out[:, i * cols : (i + 1) * cols] for i in range(len(spectra))]
 
 
-def read(ref, lane, group):
-    if len(ref.shape) == 3:
-        return ref[0, pl.ds(lane, ref.shape[1] // group, stride=group), :]
+def channel(ref, chunk, lane, group):
     count = ref.shape[2] // group
     return jnp.concatenate(
-        [ref[b, 0, pl.ds(lane, count, stride=group), :] for b in range(ref.shape[0])], axis=0
+        [ref[b, chunk, pl.ds(lane, count, stride=group), :] for b in range(ref.shape[0])], axis=0
     )
 
 
-def write(ref, lane, group, value):
-    if len(ref.shape) == 3:
-        ref[0, pl.ds(lane, ref.shape[1] // group, stride=group), :] = value
-        return
+def put(ref, chunk, lane, group, value):
     count = ref.shape[2] // group
     for b in range(ref.shape[0]):
-        ref[b, 0, pl.ds(lane, count, stride=group), :] = value[b * count : (b + 1) * count]
-
-
-def kernel(group, a, b, w1h, w1l, w2h, w2l, w3h, w3l, w4h, w4l, ct, st, out):
-    cos_t, sin_t = ct[...], st[...]
-    first, second = (w1h[...], w1l[...]), (w2h[...], w2l[...])
-    third, last = (w3h[...], w3l[...]), (w4h[...], w4l[...])
-    count = 2 if group % 2 == 0 else 1
-
-    def step(i, carry):
-        lanes = [i * count + j for j in range(count)]
-        xs = [read(a, lane, group) for lane in lanes] + [read(b, lane, group) for lane in lanes]
-        specs = forward(xs, first, second, cos_t, sin_t)
-        prods = []
-        for (a_re, a_im), (b_re, b_im) in zip(specs[:count], specs[count:]):
-            prods.append((a_re * b_re + a_im * b_im, a_re * b_im - a_im * b_re))
-        for lane, value in zip(lanes, backward(prods, third, last, cos_t, sin_t)):
-            write(out, lane, group, value)
-        return carry
-
-    lax.fori_loop(0, group // count, step, 0)
-
-
-def correlate(a, b, out_shape, group, name, tabs):
-    groups = b.shape[1]
-
-    def spec(shape):
-        if len(shape) == 3:
-            return pl.BlockSpec((1, *shape[1:]), lambda i: (i, 0, 0))
-        return pl.BlockSpec((shape[0], 1, *shape[2:]), lambda i: (0, i, 0, 0))
-
-    rows, cols = tabs[-1].shape
-    flops = 2 * 3 * groups * group * rows * cols * 3 * (2 * rows + 4 * cols)
-    return pl.pallas_call(
-        functools.partial(kernel, group),
-        grid=(groups,),
-        in_specs=[spec(a.shape), spec(b.shape)]
-        + [pl.BlockSpec(t.shape, lambda i: (0, 0)) for t in tabs],
-        out_specs=spec(out_shape),
-        out_shape=jax.ShapeDtypeStruct(out_shape, jnp.float32),
-        compiler_params=pltpu.CompilerParams(vmem_limit_bytes=56 * 1024 * 1024),
-        cost_estimate=pl.CostEstimate(
-            flops=flops, bytes_accessed=3 * 4 * a.size, transcendentals=0
-        ),
-        name=name,
-    )(a, b, *tabs)
+        ref[b, chunk, pl.ds(lane, count, stride=group), :] = value[b * count : (b + 1) * count]
+
+
+def conjugate(left, right):
+    (a_re, a_im), (b_re, b_im) = left, right
+    return a_re * b_re + a_im * b_im, a_re * b_im - a_im * b_re
 
 
 MESH = pl.DeviceIdType.MESH
@@ -262,53 +207,369 @@
     )(block)
 
 
+def block_kernel(
+    parts, group, nb, sig_in, cot_in, first_t, mix, rates, gains,
+    w1h, w1l, w2h, w2l, w3h, w3l, w4h, w4l, ct, st,
+    v1h, v1l, v4h, v4l, cv, sv,
+    in_out, filt_out, raw_out, basis_out, slope_out, embed_out, norm_out,
+    cot_buf, sig_buf, ig_buf, late_cot, late_sig, raw_buf, basis_buf, slope_buf, embed_buf,
+    zero_buf, inverse,
+    cot_got, sig_got, late_cot_got, late_sig_got, ig_got,
+    cot_sent, sig_sent, late_sent, ig_sent, late_ig_sent, done,
+):
+    me, my_chan = lax.axis_index("batch"), lax.axis_index("chan")
+    half = parts // 2
+    late = me >= half
+    groups = cot_buf.shape[1]
+    length = basis_buf.shape[1]
+    padded = groups * 8
+    barrier = pltpu.get_barrier_semaphore()
+    for k in range(1, parts):
+        peer = lax.rem(me + k, parts)
+        pl.semaphore_signal(barrier, inc=1, device_id=(peer, my_chan), device_id_type=MESH)
+    pl.semaphore_wait(barrier, parts - 1)
+
+    def send(src, dst, sent, got, peer):
+        pltpu.make_async_remote_copy(
+            src_ref=src,
+            dst_ref=dst,
+            send_sem=sent,
+            recv_sem=got,
+            device_id=(peer, my_chan),
+            device_id_type=MESH,
+        ).start()
+
+    def settle(ref, sem):
+        pltpu.make_async_copy(ref, ref, sem).wait()
+
+    for g in range(groups):
+        pltpu.make_async_copy(cot_in.at[me, g], cot_buf.at[me, g], cot_got.at[g]).start()
+        pltpu.make_async_copy(sig_in.at[me, g], sig_buf.at[me, g], sig_got.at[g]).start()
+
+    @pl.when(late)
+    def _():
+        own = me - half
+        for g in range(groups):
+            pltpu.make_async_copy(cot_in.at[own, g], late_cot.at[own, g], late_cot_got.at[g]).start()
+            pltpu.make_async_copy(sig_in.at[own, g], late_sig.at[own, g], late_sig_got.at[g]).start()
+            for k in range(1, half):
+                to = lax.rem(own + k, half)
+                send(cot_in.at[to, g], late_cot.at[own, g], late_sent, late_cot_got.at[g], to + half)
+                send(sig_in.at[to, g], late_sig.at[own, g], late_sent, late_sig_got.at[g], to + half)
+            for k in range(1, parts):
+                to = lax.rem(me + k, parts)
+                send(cot_in.at[to, g], cot_buf.at[me, g], cot_sent, cot_got.at[g], to)
+        for g in range(groups):
+            for k in range(1, half):
+                to = lax.rem(own + k, half) + half
+                send(sig_in.at[to, g], sig_buf.at[me, g], sig_sent, sig_got.at[g], to)
+
+    @pl.when(jnp.logical_not(late))
+    def _():
+        for g in range(groups):
+            for k in range(1, parts):
+                to = lax.rem(me + k, parts)
+                send(cot_in.at[to, g], cot_buf.at[me, g], cot_sent, cot_got.at[g], to)
+        for g in range(groups):
+            for k in range(1, parts):
+                to = lax.rem(me + k, parts)
+                send(sig_in.at[to, g], sig_buf.at[me, g], sig_sent, sig_got.at[g], to)
+        sig_buf[half:] = jnp.zeros((parts - half, *sig_buf.shape[1:]), jnp.float32)
+
+    zero_buf[...] = jnp.zeros(zero_buf.shape, jnp.float32)
+
+    other = lax.rem(me + half, parts)
+    mine = pl.ds(pl.multiple_of(me * padded, 8), padded)
+    theirs = pl.ds(pl.multiple_of(other * padded, 8), padded)
+    weights = split(jnp.concatenate([mix[mine, :], mix[theirs, :]], axis=0))
+    rate = jnp.concatenate([rates[mine, :], rates[theirs, :]], axis=0)[:, :1]
+    tile = 512 if length % 512 == 0 else LANES
+    width = tile // LANES
+
+    def generate(t, total):
+        start = pl.multiple_of(t * tile, tile)
+        spot = (start + lax.broadcasted_iota(jnp.int32, (nb, tile), 1)).astype(jnp.float32)
+        band = (lax.broadcasted_iota(jnp.int32, (nb, tile), 0) + 1).astype(jnp.float32)
+        turn = band * spot * (1.0 / length)
+        sines, cosines = sincos((turn - jnp.floor(turn)) * (2.0 * math.pi))
+        line = (start + lax.broadcasted_iota(jnp.int32, (8, tile), 1)).astype(jnp.float32) / length
+        line = jnp.where(lax.broadcasted_iota(jnp.int32, (8, tile), 0) == 0, line, 0.0)
+        embed = jnp.concatenate([cosines, sines, line], axis=0)
+        before = jnp.dot(
+            first_t[...], embed, precision=exact, preferred_element_type=jnp.float32
+        )
+        basis, slope = sincos(before)
+        embed_buf[:, pl.ds(start, tile)] = embed
+        basis_buf[:, pl.ds(start, tile)] = basis
+        slope_buf[:, pl.ds(start, tile)] = slope
+        raw = jnp.exp(-rate * line[:1]) * product(weights, split(basis))
+        for j in range(width):
+            piece = raw[:, j * LANES : (j + 1) * LANES]
+            total = total + piece * piece
+            row = pl.ds(pl.multiple_of((t * width + j) * 8, 8), 8)
+            for h in range(2 * groups):
+                raw_buf[h, row, :] = piece[h * 8 : (h + 1) * 8]
+        return total
+
+    total = lax.fori_loop(
+        0, length // tile, generate, jnp.zeros((2 * padded, LANES), jnp.float32)
+    )
+    norm = jnp.sqrt(jnp.sum(total, axis=1, keepdims=True) + epsilon)
+    norm_out[...] = jnp.broadcast_to(norm, norm_out.shape)
+    inverse[...] = jnp.broadcast_to(1.0 / norm, inverse.shape)
+    outputs = ((raw_buf, raw_out), (basis_buf, basis_out), (slope_buf, slope_out), (embed_buf, embed_out))
+    for i, (src, dst) in enumerate(outputs):
+        pltpu.make_async_copy(src, dst, done.at[i]).start()
+
+    second, third = (w2h[...], w2l[...]), (w3h[...], w3l[...])
+    count = 2 if group % 2 == 0 else 1
+    pairs = group // count
+    rows = raw_buf.shape[1] // 8
+
+    @pl.when(late)
+    def _():
+        own = me - half
+        first, last = (v1h[...], v1l[...]), (v4h[...], v4l[...])
+        cos_t, sin_t = cv[...], sv[...]
+
+        def chunk(g, carry):
+            settle(late_cot.at[:, g], late_cot_got.at[g])
+            settle(late_sig.at[:, g], late_sig_got.at[g])
+
+            def step(p, carry):
+                lanes = [p * count + j for j in range(count)]
+                cots = [channel(late_cot, g, lane, group) for lane in lanes]
+                sigs = [channel(late_sig, g, lane, group) for lane in lanes]
+                raws = [
+                    raw_buf[groups + g, pl.ds(lane, rows // 2, stride=8), :] for lane in lanes
+                ]
+                specs = forward(cots + sigs + raws, first, second, cos_t, sin_t)
+                prods = [conjugate(specs[2 * count + j], specs[j]) for j in range(count)]
+                prods += [conjugate(specs[count + j], specs[j]) for j in range(count)]
+                values = backward(prods, third, last, cos_t, sin_t)
+                for j, lane in enumerate(lanes):
+                    at = pl.ds(padded + g * 8 + lane, 1)
+                    gain = gains[pl.ds(other * padded + g * 8 + lane, 1), :]
+                    put(late_cot, g, lane, group, values[j] * inverse[at, :] + gain * cots[j])
+                    put(late_sig, g, lane, group, values[count + j])
+                return carry
+
+            lax.fori_loop(0, pairs, step, 0)
+            pltpu.make_async_copy(late_cot.at[own, g], in_out.at[own, g], ig_got).start()
+            for k in range(1, half):
+                to = lax.rem(own + k, half)
+                send(late_cot.at[to, g], in_out.at[own, g], late_ig_sent, ig_got, to + half)
+            pltpu.make_async_copy(late_sig.at[:, g], filt_out.at[groups + g, pl.ds(0, half)], done.at[4]).start()
+            pltpu.make_async_copy(zero_buf, filt_out.at[groups + g, pl.ds(half, half)], done.at[5]).start()
+            return carry
+
+        lax.fori_loop(0, groups, chunk, 0)
+
+    @pl.when(jnp.logical_not(late))
+    def _():
+        for g in range(groups):
+            pltpu.make_async_copy(zero_buf, filt_out.at[groups + g, pl.ds(0, half)], done.at[4]).start()
+            pltpu.make_async_copy(zero_buf, filt_out.at[groups + g, pl.ds(half, half)], done.at[5]).start()
+
+    first, last = (w1h[...], w1l[...]), (w4h[...], w4l[...])
+    cos_t, sin_t = ct[...], st[...]
+
+    def input_chunk(g, carry):
+        settle(cot_buf.at[:, g], cot_got.at[g])
+
+        def step(p, carry):
+            lanes = [p * count + j for j in range(count)]
+            cots = [channel(cot_buf, g, lane, group) for lane in lanes]
+            raws = [raw_buf[g, pl.ds(lane, rows, stride=8), :] for lane in lanes]
+            specs = forward(raws + cots, first, second, cos_t, sin_t)
+            prods = [conjugate(specs[j], specs[count + j]) for j in range(count)]
+            values = backward(prods, third, last, cos_t, sin_t)
+            for j, lane in enumerate(lanes):
+                gain = gains[pl.ds(me * padded + g * 8 + lane, 1), :]
+                scale = inverse[pl.ds(g * 8 + lane, 1), :]
+                put(ig_buf, g, lane, group, values[j] * scale + gain * cots[j])
+            return carry
+
+        lax.fori_loop(0, pairs, step, 0)
+        pltpu.make_async_copy(ig_buf.at[me, g], in_out.at[me, g], ig_got).start()
+
+        @pl.when(late)
+        def _():
+            for k in range(1, parts):
+                to = lax.rem(me + k, parts)
+                send(ig_buf.at[to, g], in_out.at[me, g], ig_sent, ig_got, to)
+
+        @pl.when(jnp.logical_not(late))
+        def _():
+            for k in range(1, half):
+                to = lax.rem(me + k, half)
+                send(ig_buf.at[to, g], in_out.at[me, g], ig_sent, ig_got, to)
+
+        return carry
+
+    lax.fori_loop(0, groups, input_chunk, 0)
+
+    def filter_chunk(g, carry):
+        @pl.when(late)
+        def _():
+            settle(sig_buf.at[:, g], sig_got.at[g])
+
+        @pl.when(jnp.logical_not(late))
+        def _():
+            settle(sig_buf.at[pl.ds(0, half), g], sig_got.at[g])
+
+        def step(p, carry):
+            lanes = [p * count + j for j in range(count)]
+            cots = [channel(cot_buf, g, lane, group) for lane in lanes]
+            sigs = [channel(sig_buf, g, lane, group) for lane in lanes]
+            specs = forward(sigs + cots, first, second, cos_t, sin_t)
+            prods = [conjugate(specs[j], specs[count + j]) for j in range(count)]
+            values = backward(prods, third, last, cos_t, sin_t)
+            for j, lane in enumerate(lanes):
+                put(sig_buf, g, lane, group, values[j])
+            return carry
+
+        lax.fori_loop(0, pairs, step, 0)
+        pltpu.make_async_copy(sig_buf.at[:, g], filt_out.at[g], done.at[6]).start()
+        return carry
+
+    lax.fori_loop(0, groups, filter_chunk, 0)
+
+    for i, (src, dst) in enumerate(outputs):
+        settle(dst, done.at[i])
+    settle(filt_out.at[pl.ds(0, groups), pl.ds(0, half)], done.at[4])
+    settle(filt_out.at[pl.ds(0, groups), pl.ds(0, half)], done.at[5])
+    settle(filt_out.at[pl.ds(0, groups)], done.at[6])
+    settle(cot_in.at[pl.ds(0, parts - 1)], cot_sent)
+    settle(in_out, ig_got)
+
+    @pl.when(late)
+    def _():
+        settle(cot_in.at[pl.ds(0, 2 * (half - 1))], late_sent)
+        settle(cot_in.at[pl.ds(0, half - 1)], late_ig_sent)
+        settle(cot_in.at[pl.ds(0, half - 1)], sig_sent)
+        settle(cot_in.at[pl.ds(0, parts - 1)], ig_sent)
+
+    @pl.when(jnp.logical_not(late))
+    def _():
+        settle(cot_in.at[pl.ds(0, parts - 1)], sig_sent)
+        settle(cot_in.at[pl.ds(0, half - 1)], ig_sent)
+
+
+def run_block(sig, cot, first_t, mix, rates, gains, group, length):
+    parts, groups, run, _ = sig.shape
+    half = parts // 2
+    rows = length // LANES
+    nb = (first_t.shape[1] - 8) // 2
+    order = first_t.shape[0]
+    tabs = tables(rows, LANES)
+    small = tables(rows // 2, LANES)
+    small = (*small[:2], *small[6:])
+    hbm = pl.BlockSpec(memory_space=pl.ANY)
+    vmem = pl.BlockSpec(memory_space=pltpu.VMEM)
+    dma = pltpu.SemaphoreType.DMA
+    f32 = jnp.float32
+    pieces = (first_t, mix, rates, gains, *tabs, *small)
+    return pl.pallas_call(
+        functools.partial(block_kernel, parts, group, nb),
+        in_specs=[hbm, hbm] + [vmem] * len(pieces),
+        out_specs=[hbm] * 6 + [vmem],
+        out_shape=[
+            jax.ShapeDtypeStruct(sig.shape, f32),
+            jax.ShapeDtypeStruct((2 * groups, parts, run, LANES), f32),
+            jax.ShapeDtypeStruct((2 * groups, rows * 8, LANES), f32),
+            jax.ShapeDtypeStruct((order, length), f32),
+            jax.ShapeDtypeStruct((order, length), f32),
+            jax.ShapeDtypeStruct((first_t.shape[1], length), f32),
+            jax.ShapeDtypeStruct((2 * groups * 8, LANES), f32),
+        ],
+        scratch_shapes=[
+            pltpu.VMEM(sig.shape, f32),
+            pltpu.VMEM(sig.shape, f32),
+            pltpu.VMEM(sig.shape, f32),
+            pltpu.VMEM((half, groups, run, LANES), f32),
+            pltpu.VMEM((half, groups, run, LANES), f32),
+            pltpu.VMEM((2 * groups, rows * 8, LANES), f32),
+            pltpu.VMEM((order, length), f32),
+            pltpu.VMEM((order, length), f32),
+            pltpu.VMEM((first_t.shape[1], length), f32),
+            pltpu.VMEM((half, run, LANES), f32),
+            pltpu.VMEM((2 * groups * 8, LANES), f32),
+            dma((groups,)),
+            dma((groups,)),
+            dma((groups,)),
+            dma((groups,)),
+            dma,
+            dma,
+            dma,
+            dma,
+            dma,
+            dma,
+            dma((7,)),
+        ],
+        compiler_params=pltpu.CompilerParams(
+            collective_id=1, has_side_effects=True, vmem_limit_bytes=67043328
+        ),
+        name="block",
+    )(sig, cot, *pieces)
+
+
 def local(signal, cotangent, first_layer, second_layer, decay_rate, skip_gain):
     parts = lax.axis_size("batch")
     place = lax.axis_index("batch")
     width_dev, local_len = signal.shape
+    bands, order = first_layer.shape
     length = local_len * parts
     factor = 1.0 / math.sqrt(length)
     narrow = width_dev // parts
     group = min(8, narrow)
     groups = narrow // group
     rows = length // LANES
-    tabs = tables(rows, LANES)
-
-    def spread(x):
+    nb = bands // 2
+
+    def tiles(x):
         x = x.reshape(parts, groups, group, local_len // LANES, LANES)
-        x = x.transpose(0, 1, 3, 2, 4).reshape(parts, groups, -1, LANES)
-        return lax.all_to_all(x, "batch", split_axis=0, concat_axis=0, tiled=True)
-
-    def tiled(x):
-        x = x.reshape(groups, group, rows, LANES).transpose(0, 2, 1, 3)
-        return x.reshape(groups, rows * group, LANES)
-
-    cot = spread(cotangent)
-    positions = jnp.arange(length, dtype=jnp.int32)
-    columns = lax.dynamic_slice_in_dim(second_layer, place * narrow, narrow, 1)
-    rates = lax.dynamic_slice_in_dim(decay_rate, place * narrow, narrow, 0)
-    gains = lax.dynamic_slice_in_dim(skip_gain, place * narrow, narrow, 0)
-    embed = features(positions, length, first_layer.shape[0] // 2)
-    before = jnp.dot(first_layer.T, embed, precision=exact)
-    basis, slope = sincos(before)
-    fraction = positions.astype(jnp.float32) / length
+        return x.transpose(0, 1, 3, 2, 4).reshape(parts, groups, -1, LANES)
+
+    def fill(x):
+        x = x.reshape(parts * groups, group, -1)
+        x = jnp.pad(x, ((0, 0), (0, 8 - group), (0, 0)))
+        return x.reshape(parts * groups * 8, -1)
+
+    first_t = jnp.concatenate([first_layer[1:], first_layer[:1]], axis=0)
+    first_t = jnp.pad(first_t, ((0, 7), (0, 0))).T
+    spread = lambda x: jnp.broadcast_to(fill(x), (parts * groups * 8, LANES))
+    in_grad, filt_grad, shaped, basis, slope, embed, norms = run_block(
+        tiles(signal),
+        tiles(cotangent),
+        first_t,
+        fill(second_layer.T),
+        spread(decay_rate),
+        spread(skip_gain),
+        group,
+        length,
+    )
+    input_grad = in_grad.reshape(parts, groups, local_len // LANES, group, LANES)
+    input_grad = input_grad.transpose(0, 1, 3, 2, 4).reshape(width_dev, local_len)
+
+    def flat(x, q):
+        x = x.reshape(2 * groups, rows, q, LANES).transpose(0, 2, 1, 3)[:, :group]
+        return x.reshape(2 * narrow, length)
+
+    other = (place + parts // 2) % parts
+
+    def both(x):
+        own = lax.dynamic_slice_in_dim(x, place * narrow, narrow, 0)
+        return jnp.concatenate([own, lax.dynamic_slice_in_dim(x, other * narrow, narrow, 0)])
+
+    columns = both(second_layer.T).T
+    rates = both(decay_rate)
+    norms = norms.reshape(2 * groups, 8, LANES)[:, :group, :1].reshape(2 * narrow, 1)
+    fraction = jnp.arange(length, dtype=jnp.int32).astype(jnp.float32) / length
     window = jnp.exp(-rates[:, None] * fraction[None, :])
-    shaped = window * jnp.dot(columns.T, basis, precision=precise)
-    norms = jnp.sqrt(jnp.sum(shaped * shaped, axis=1, keepdims=True) + epsilon)
+    dfilt = factor * flat(filt_grad, group)
+    shaped = flat(shaped, 8)
     filt = shaped / norms
-    taps = tiled(filt + jnp.where(positions[None, :] == 0, gains[:, None], 0.0))
-    cot, signal, taps, basis, slope = lax.optimization_barrier((cot, signal, taps, basis, slope))
-    val = spread(signal)
-    in_grad = correlate(taps, cot, cot.shape, group, "input_grad", tabs)
-    val, in_grad = lax.optimization_barrier((val, in_grad))
-    input_grad = lax.all_to_all(in_grad, "batch", split_axis=0, concat_axis=0, tiled=True)
-    filt_grad = correlate(val, cot, taps.shape, group, "filter_grad", tabs)
-    input_grad = input_grad.reshape(parts, groups, local_len // LANES, group, LANES)
-    input_grad = input_grad.transpose(0, 1, 3, 2, 4).reshape(width_dev, local_len)
-    filt_grad = filt_grad.reshape(groups, rows, group, LANES).transpose(0, 2, 1, 3)
-    dfilt = factor * filt_grad.reshape(narrow, length)
-    skip_part = (cot * val).reshape(parts, groups, local_len // LANES, group, LANES)
-    skip_part = factor * jnp.sum(skip_part, axis=(0, 2, 4)).reshape(narrow)
     project = jnp.sum(filt * dfilt, axis=1, keepdims=True)
     draw = (dfilt - filt * project) / norms
     decay_part = -jnp.sum(draw * shaped * fraction[None, :], axis=1)
@@ -316,20 +577,32 @@
     second_part = jnp.dot(dmix, basis.T, precision=precise)
     dbasis = jnp.dot(columns, dmix, precision=precise)
     first_part = jnp.dot(embed, (slope * dbasis).T, precision=precise)
-    bands, order = first_layer.shape
-    left = jnp.concatenate([decay_part, skip_part])
-    left = jnp.concatenate([first_part, jnp.pad(left, (0, order - 2 * narrow))[None]], axis=0)
-    high = -(-max(bands + 1, narrow) // 8) * 8
-    left = jnp.pad(left, ((0, high - bands - 1), (0, 0)))
-    right = jnp.pad(second_part, ((0, high - narrow), (0, 0)))
+    skip_part = factor * jnp.sum(cotangent * signal, axis=1)
+    left = jnp.concatenate(
+        [
+            first_part[2 * nb : bands],
+            first_part[: 2 * nb],
+            jnp.pad(decay_part, (0, order - 2 * narrow))[None],
+            skip_part.reshape(-1, order),
+        ],
+        axis=0,
+    )
+    high = -(-max(left.shape[0], 2 * narrow) // 8) * 8
+    left = jnp.pad(left, ((0, high - left.shape[0]), (0, 0)))
+    right = jnp.pad(second_part, ((0, high - 2 * narrow), (0, 0)))
     block = jnp.concatenate([left, right], axis=1)
-    block, input_grad = lax.optimization_barrier((block, input_grad))
     shared, total = share(block, parts, lax.axis_size("chan"))
     first_grad = total[:bands, :order]
-    second_grad = shared[:, :narrow, order:].reshape(width_dev, order).T
-    decay_grad = shared[:, bands, :narrow].reshape(width_dev)
-    skip_grad = shared[:, bands, narrow : 2 * narrow].reshape(width_dev)
-    return (input_grad, first_grad, second_grad, decay_grad, skip_grad)
+
+    def merge(own, late):
+        return own + jnp.roll(late, -(parts // 2), axis=0)
+
+    second_grad = merge(shared[:, :narrow, order:], shared[:, narrow : 2 * narrow, order:])
+    second_grad = second_grad.reshape(width_dev, order).T
+    decays = shared[:, bands]
+    decay_grad = merge(decays[:, :narrow], decays[:, narrow : 2 * narrow]).reshape(width_dev)
+    skip_grad = jnp.sum(shared[:, bands + 1 : bands + 1 + width_dev // order, :order], axis=0)
+    return (input_grad, first_grad, second_grad, decay_grad, skip_grad.reshape(width_dev))
 
 
 def solution(mesh):

time: 317 us -> 325 us (1.025)
  Pallas kernels: 98.3 us -> 250 us
  waiting for transfers between devices: 131 us -> 0 us
  matrix products: 41 us -> 23.3 us
  starting transfers between devices: 16.7 us -> 0 us
  other arithmetic: 17 us -> 33.1 us
  local copies, waits for them, and re-layouts: 11.9 us -> 16.5 us
    pallas_call x2 -> x1, Pallas kernels: 86.8 us -> 228 us  [run_block(): pl.pallas_call(functools.partial(block_kernel, parts, group, nb), in_spec...]
    all_to_all x3 -> x0, waiting for transfers between devices: 131 us -> none  [the longest x2 110 us: spread(): return lax.all_to_all(x, 'batch', split_axis=0, concat_axis=0, tiled=True)]
    dot_general x2 -> x0, matrix products: 23.7 us -> none  [the longest x1 19.3 us: local(): before = jnp.dot(first_layer.T, embed, precision=exact)]
    all_to_all x3 -> x0, starting transfers between devices: 16.7 us -> none  [the longest x2 12.2 us: spread(): return lax.all_to_all(x, 'batch', split_axis=0, concat_axis=0, tiled=True)]
    mul x1 -> x3, other arithmetic: 0.01 us -> 15.1 us  [the longest x1 8.09 us: local(): dfilt = factor * flat(filt_grad, group)]
    pallas_call x1, Pallas kernels: 11.5 us -> 22.4 us  [share(): pl.pallas_call(functools.partial(share_kernel, parts, chans), in_specs=[v...]
    dot_general x1, matrix products: 3.73 us -> 9.36 us  [local(): second_part = jnp.dot(dmix, basis.T, precision=precise)]
    reduce_sum x1, other arithmetic: 2.75 us -> 7.3 us  [local(): decay_part = -jnp.sum(draw * shaped * fraction[None, :], axis=1)]
  transfers between devices with their start and end apart: 3 -> 0, of which waited for: 3 -> 0; matrix products, arithmetic and copies ran while one was open for 18% -> 0% of each run, Pallas kernels for 27% -> 0%
where the time goes in v3:
time: 325 us; the launch traced here: 324 us
  Pallas kernels  250 us (77%)
  other arithmetic  33.1 us (10%)
  matrix products  23.3 us (7%)
  local copies, waits for them, and re-layouts  16.5 us (5%)
    pallas_call x1, Pallas kernels, run_block(): pl.pallas_call(functools.partial(block_kernel, parts, group, nb), in_spec...  228 us
    pallas_call x1, Pallas kernels, share(): pl.pallas_call(functools.partial(share_kernel, parts, chans), in_specs=[v...  22.4 us
    dot_general x1, matrix products, local(): dbasis = jnp.dot(columns, dmix, precision=precise)  10.2 us
    dot_general x1, matrix products, local(): second_part = jnp.dot(dmix, basis.T, precision=precise)  9.36 us
    mul x1, other arithmetic, local(): dfilt = factor * flat(filt_grad, group)  8.09 us
    reduce_sum x1, other arithmetic, local(): decay_part = -jnp.sum(draw * shaped * fraction[None, :], axis=1)  7.3 us
    mul x1, other arithmetic, local(): dmix = draw * window  7.04 us
    reduce_sum x1, other arithmetic, local(): project = jnp.sum(filt * dfilt, axis=1, keepdims=True)  6.9 us

profile of v3, /device:TPU:0, one launch (start us, length us, event | category | flops | bytes accessed | tf_op | source)
XLA Modules:
  0.0 324.2 jit_solution(4145829971249802965)
XLA Ops:
  0.6 0.7 slice.53
  1.3 0.1 copy.28
  1.4 0.7 slice.52
  2.2 0.1 copy.32
  2.2 0.7 fusion.6.first_t
  2.9 1.6 copy.29
  4.5 1.4 broadcast_in_dim.4.rates
  6.0 1.4 broadcast_in_dim.5.gains
  7.4 228.0 %block.1 = (f32[8,4,256,128]{3,2,1,0:T(8,128)}, f32[8,8,256,128]{3,2,1,0:T(8,128)}, f32[8,2048,128]{2,1,0:T(8,128)}, f32[64,32768]{1,0:T(8,128)}, f32[64,32768]{...) custom-call(f32[8,4,256,128]{3,2,1,0:T(8,128)} %bitcast.67, f32[8,4,256,128]{3,2,1,0:T(8,128)} %bitcast.68, ...), custom_call_target="tpu_custom_call" | custom-call | tf_op jit(solution)/shard_map/block/pallas_call | solution.py:473
  235.4 8.1 %broadcast_multiply_fusion = f32[8,8,256,128]{3,2,1,0:T(8,128)} fusion(f32[8,8,256,128]{3,2,1,0:T(8,128)} %get-tuple-element.17), kind=kLoop, calls=%fused_computation.12 | loop fusion | flops 2097152 | bytes 16777216 | tf_op jit(solution)/shard_map/mul | solution.py:570
  243.6 0.1 fusion.13
  243.7 0.1 copy.33
  243.8 6.9 %multiply_reduce_fusion = f32[8,8]{1,0:T(8,128)S(1)} fusion(f32[8,8,256,128]{3,1,2,0:T(8,128)} %bitcast.64, f32[8,8]{1,0:T(8,128)S(1)} %bitcast.75, f32[8,2048,128]{2,1,0:T(8,128)} %get-tuple-element.18), kind=kLoop, calls=%fused_computation.10 | loop fusion | flops 6291392 | bytes 16777728 | tf_op jit(solution)/shard_map/reduce_sum | solution.py:573
  250.7 0.1 mul.99
  250.9 7.0 %fusion.3 = f32[64,32768]{1,0:T(8,128)S(1)} fusion(f32[64,32768]{1,0:T(8,128)} %bitcast.65, f32[8,2048,128]{2,1,0:T(8,128)} %get-tuple-element.18, f32[32768]{0:T(1024)S(1)} %convert_multiply_fusion.1, f32[64]{0:T(128)S(1)} %maximum_negate_fusion, f32[64]{0:T(128)S(1)} %mul.99, f32[64]{0:T(128)S(1)} %div.37), kind=kLoop, calls=%fused_computation.5 | loop fusion | flops 12582912 | bytes 25297664 | tf_op jit(solution)/shard_map/mul | solution.py:576
  258.0 9.4 %fusion.15 = f32[64,64]{1,0:T(8,128)S(1)} fusion(f32[64,32768]{1,0:T(8,128)S(1)} %fusion.3, f32[64,32768]{1,0:T(8,128)} %get-tuple-element.20), kind=kOutput, calls=%fused_computation.38 | convolution fusion | flops 805306368 | bytes 16793600 | tf_op jit(solution)/shard_map/dot_general | solution.py:577
  267.4 0.5 multiply_reduce_fusion.1
  267.9 0.1 mul.115
  268.0 7.3 %fusion.5 = f32[8,8]{1,0:T(8,128)S(1)} fusion(f32[8,2048,128]{2,1,0:T(8,128)} %get-tuple-element.18, f32[8,8,256,128]{3,1,2,0:T(8,128)} %bitcast.66, f32[256,128]{1,0:T(8,128)S(1)} %convert_multiply_fusion, f32[8,8]{1,0:T(8,128)S(1)} %multiply_reduce_fusion, f32[8,8]{1,0:T(8,128)S(1)} %bitcast.76), kind=kLoop, calls=%fused_computation.9 | loop fusion | flops 14680000 | bytes 16909056 | tf_op jit(solution)/shard_map/reduce_sum | solution.py:575
  275.5 10.2 %convolution_multiply_fusion = f32[64,32768]{1,0:T(8,128)S(1)} fusion(f32[64,32768]{1,0:T(8,128)} %get-tuple-element.16, f32[64,32768]{1,0:T(8,128)} %copy-done, f32[32,64]{0,1:T(8,128)S(1)} %get-tuple-element.26, f32[32,64]{0,1:T(8,128)S(1)} %get-tuple-element.25), kind=kOutput, calls=%fused_computation | convolution fusion | flops 807407616 | bytes 25182208 | tf_op jit(solution)/shard_map/dot_general | solution.py:578
  285.7 3.7 %fusion.14 = f32[40,64]{1,0:T(8,128)S(1)} fusion(f32[40,32768]{1,0:T(8,128)S(1)} %bitcast.70, f32[64,32768]{1,0:T(8,128)S(1)} %convolution_multiply_fusion), kind=kOutput, calls=%fused_computation.37 | convolution fusion | flops 503316480 | bytes 13641728 | tf_op jit(solution)/shard_map/dot_general | solution.py:579
  289.5 0.7 pad_maximum_fusion.mine
  290.2 22.4 %share.1 = (f32[8,64,128]{2,1,0:T(8,128)}, f32[64,128]{1,0:T(8,128)}) custom-call(f32[64,128]{1,0:T(8,128)} %pad_maximum_fusion.mine), custom_call_target="tpu_custom_call" | custom-call | tf_op jit(solution)/shard_map/share/pallas_call | solution.py:188
  312.6 1.3 slice.57
  314.0 1.0 fusion.11
  314.9 1.0 maximum_add_fusion
  315.9 0.7 copy.31
  316.7 0.8 slice.61
  317.5 0.6 reshape.144
  318.2 0.8 slice_reduce_fusion
  318.9 0.6 reshape.145
  319.6 4.7 %copy.35 = f32[256,4096]{1,0:T(8,128)} copy(f32[256,4096]{1,0:T(8,128)} %bitcast.71) | data formatting | bytes 8388608
  (30 shorter events, 0.5 us)
Async XLA Ops:
  235.4 8.2 %copy-start.5 = (f32[256]{0:T(256)S(1)}, f32[256]{0:T(256)}, u32[]{:S(2)}) copy-start(f32[256]{0:T(256)} %param.26) | copy-start | bytes 3076
  235.4 8.3 %copy-start.4 = (f32[64,128]{1,0:T(8,128)S(1)}, f32[64,128]{1,0:T(8,128)}, u32[]{:S(2)}) copy-start(f32[64,128]{1,0:T(8,128)} %get-tuple-element.19) | copy-start | bytes 98308
  258.0 9.4 %copy-start = (f32[64,32768]{1,0:T(8,128)}, f32[64,32768]{1,0:T(8,128)S(1)}, u32[]{:S(2)}) copy-start(f32[64,32768]{1,0:T(8,128)S(1)} %fusion.3) | copy-start | bytes 25165828
  258.0 9.4 %copy-start.1 = (f32[256,4096]{1,0:T(8,128)S(1)}, f32[256,4096]{1,0:T(8,128)}, u32[]{:S(2)}) copy-start(f32[256,4096]{1,0:T(8,128)} %param.22) | copy-start | bytes 12582916
  258.0 9.4 %copy-start.2 = (f32[256,4096]{1,0:T(8,128)S(1)}, f32[256,4096]{1,0:T(8,128)}, u32[]{:S(2)}) copy-start(f32[256,4096]{1,0:T(8,128)} %param.23) | copy-start | bytes 12582916
  268.0 7.4 %copy-start.3 = (f32[64,256]{1,0:T(8,128)S(1)}, f32[64,256]{1,0:T(8,128)}, u32[]{:S(2)}) copy-start(f32[64,256]{1,0:T(8,128)} %param.25) | copy-start | bytes 196612
  268.0 17.7 %slice-start = ((s8[5242880]{0:T(1024)(128)(4,1)}), s8[1048576]{0:T(1024)(128)(4,1)S(1)}, s32[]{:S(2)}) async-start(s8[5242880]{0:T(1024)(128)(4,1)} %bitcast.69), calls=%async_computation | async-start | bytes 2097152
  275.5 10.3 %slice-start.1 = ((s8[5242880]{0:T(1024)(128)(4,1)}), s8[4194304]{0:T(1024)(128)(4,1)S(1)}, s32[]{:S(2)}) async-start(s8[5242880]{0:T(1024)(128)(4,1)} %bitcast.69), calls=%async_computation.1 | async-start | bytes 8388608

commit v4 on v3

--- a/solution.py
+++ b/solution.py
@@ -124,98 +124,15 @@
 MESH = pl.DeviceIdType.MESH
 
 
-def share_kernel(parts, chans, mine, shared, total, slots, partial, sums, sends, arrivals, sends2, arrivals2):
-    me, my_chan = lax.axis_index("batch"), lax.axis_index("chan")
-    barrier = pltpu.get_barrier_semaphore()
-    for k in range(1, parts):
-        peer = lax.rem(me + k, parts)
-        pl.semaphore_signal(barrier, inc=1, device_id=(peer, my_chan), device_id_type=MESH)
-    for k in range(1, chans):
-        peer = lax.rem(my_chan + k, chans)
-        pl.semaphore_signal(barrier, inc=1, device_id=(me, peer), device_id_type=MESH)
-    pl.semaphore_wait(barrier, parts + chans - 2)
-    copies = []
-    for k in range(1, parts):
-        copies.append(
-            pltpu.make_async_remote_copy(
-                src_ref=mine,
-                dst_ref=slots.at[k],
-                send_sem=sends.at[k],
-                recv_sem=arrivals.at[k],
-                device_id=(lax.rem(me + k, parts), my_chan),
-                device_id_type=MESH,
-            )
-        )
-        copies[-1].start()
-    slots[0] = mine[...]
-    for copy in copies:
-        copy.wait_recv()
-    acc = jnp.zeros(mine.shape, jnp.float32)
-    for b in range(parts):
-        block = slots[lax.rem(me + parts - b, parts)]
-        shared[b] = block
-        acc = acc + block
-    partial[...] = acc
-    for copy in copies:
-        copy.wait_send()
-    copies = []
-    for k in range(1, chans):
-        copies.append(
-            pltpu.make_async_remote_copy(
-                src_ref=partial,
-                dst_ref=sums.at[k],
-                send_sem=sends2.at[k],
-                recv_sem=arrivals2.at[k],
-                device_id=(me, lax.rem(my_chan + k, chans)),
-                device_id_type=MESH,
-            )
-        )
-        copies[-1].start()
-    sums[0] = acc
-    for copy in copies:
-        copy.wait_recv()
-    acc = jnp.zeros_like(acc)
-    for c in range(chans):
-        acc = acc + sums[lax.rem(my_chan + chans - c, chans)]
-    total[...] = acc
-    for copy in copies:
-        copy.wait_send()
-
-
-def share(block, parts, chans):
-    vmem = pl.BlockSpec(memory_space=pltpu.VMEM)
-    dma = pltpu.SemaphoreType.DMA
-    return pl.pallas_call(
-        functools.partial(share_kernel, parts, chans),
-        in_specs=[vmem],
-        out_specs=[vmem, vmem],
-        out_shape=[
-            jax.ShapeDtypeStruct((parts, *block.shape), jnp.float32),
-            jax.ShapeDtypeStruct(block.shape, jnp.float32),
-        ],
-        scratch_shapes=[
-            pltpu.VMEM((parts, *block.shape), jnp.float32),
-            pltpu.VMEM(block.shape, jnp.float32),
-            pltpu.VMEM((chans, *block.shape), jnp.float32),
-            dma((parts,)),
-            dma((parts,)),
-            dma((chans,)),
-            dma((chans,)),
-        ],
-        compiler_params=pltpu.CompilerParams(collective_id=0, has_side_effects=True),
-        name="share",
-    )(block)
-
-
 def block_kernel(
-    parts, group, nb, sig_in, cot_in, first_t, mix, rates, gains,
+    parts, chans, group, nb, sig_in, cot_in, first_t, mix, mix_t, rates, gains,
     w1h, w1l, w2h, w2l, w3h, w3l, w4h, w4l, ct, st,
     v1h, v1l, v4h, v4l, cv, sv,
-    in_out, filt_out, raw_out, basis_out, slope_out, embed_out, norm_out,
+    in_out, shared, whole,
     cot_buf, sig_buf, ig_buf, late_cot, late_sig, raw_buf, basis_buf, slope_buf, embed_buf,
-    zero_buf, inverse,
+    inverse, project, skip, decay, second_buf, first_buf, mine_buf, slots, partial, sums,
     cot_got, sig_got, late_cot_got, late_sig_got, ig_got,
-    cot_sent, sig_sent, late_sent, ig_sent, late_ig_sent, done,
+    cot_sent, sig_sent, late_sent, ig_sent, late_ig_sent, sends, arrivals, sends2, arrivals2,
 ):
     me, my_chan = lax.axis_index("batch"), lax.axis_index("chan")
     half = parts // 2
@@ -227,7 +144,10 @@
     for k in range(1, parts):
         peer = lax.rem(me + k, parts)
         pl.semaphore_signal(barrier, inc=1, device_id=(peer, my_chan), device_id_type=MESH)
-    pl.semaphore_wait(barrier, parts - 1)
+    for k in range(1, chans):
+        peer = lax.rem(my_chan + k, chans)
+        pl.semaphore_signal(barrier, inc=1, device_id=(me, peer), device_id_type=MESH)
+    pl.semaphore_wait(barrier, parts + chans - 2)
 
     def send(src, dst, sent, got, peer):
         pltpu.make_async_remote_copy(
@@ -276,8 +196,11 @@
                 send(sig_in.at[to, g], sig_buf.at[me, g], sig_sent, sig_got.at[g], to)
         sig_buf[half:] = jnp.zeros((parts - half, *sig_buf.shape[1:]), jnp.float32)
 
-    zero_buf[...] = jnp.zeros(zero_buf.shape, jnp.float32)
-
+    skip[...] = jnp.zeros(skip.shape, jnp.float32)
+    project[...] = jnp.zeros(project.shape, jnp.float32)
+    decay[...] = jnp.zeros(decay.shape, jnp.float32)
+    second_buf[...] = jnp.zeros(second_buf.shape, jnp.float32)
+    first_buf[...] = jnp.zeros(first_buf.shape, jnp.float32)
     other = lax.rem(me + half, parts)
     mine = pl.ds(pl.multiple_of(me * padded, 8), padded)
     theirs = pl.ds(pl.multiple_of(other * padded, 8), padded)
@@ -315,11 +238,81 @@
         0, length // tile, generate, jnp.zeros((2 * padded, LANES), jnp.float32)
     )
     norm = jnp.sqrt(jnp.sum(total, axis=1, keepdims=True) + epsilon)
-    norm_out[...] = jnp.broadcast_to(norm, norm_out.shape)
     inverse[...] = jnp.broadcast_to(1.0 / norm, inverse.shape)
-    outputs = ((raw_buf, raw_out), (basis_buf, basis_out), (slope_buf, slope_out), (embed_buf, embed_out))
-    for i, (src, dst) in enumerate(outputs):
-        pltpu.make_async_copy(src, dst, done.at[i]).start()
+    factor = 1.0 / math.sqrt(length)
+    long = 1024 if length % 1024 == 0 else LANES
+
+    def total_of(ref, base):
+        return jnp.sum(ref[pl.ds(base, padded), :], axis=1, keepdims=True)
+
+    def functionals(lags, base, weights_t):
+        scale = inverse[pl.ds(base, padded), :][:, :1]
+        weight = factor * scale
+        shift = -weight * scale * scale * total_of(project, base)
+        speed = rate[base : base + padded]
+        mixer = split(weights_t)
+        per = long // LANES
+        run = lags.shape[2] // group
+        first_chunk = base // 8
+
+        def gather(t, fetch):
+            lines = []
+            for h in range(groups):
+                lines.append(jnp.concatenate([fetch(h, t * per + j) for j in range(per)], axis=1))
+            return jnp.concatenate(lines, axis=0)
+
+        def lag_tile(h, r):
+            b = lax.div(r, run)
+            at = (r - b * run) * group
+            if group == 8:
+                at = pl.multiple_of(at, 8)
+            value = lags[b, h, pl.ds(at, group), :]
+            if group < 8:
+                value = jnp.concatenate(
+                    [value, jnp.zeros((8 - group, LANES), jnp.float32)], axis=0
+                )
+            return value
+
+        def raw_tile(h, r):
+            return raw_buf[first_chunk + h, pl.ds(pl.multiple_of(r * 8, 8), 8), :]
+
+        def nt(left, right):
+            dims = (((1,), (1,)), ((), ()))
+            one = lambda x, y: lax.dot_general(x, y, dims, preferred_element_type=jnp.float32)
+            return one(left[0], right[0]) + (one(left[1], right[0]) + one(left[0], right[1]))
+
+        def step(lagged, t, sums_so_far):
+            second_sum, first_sum, decay_sum = sums_so_far
+            start = pl.multiple_of(t * long, long)
+            embed = embed_buf[:, pl.ds(start, long)]
+            line = embed[2 * nb : 2 * nb + 1]
+            raw = gather(t, raw_tile)
+            draw = raw * shift
+            if lagged:
+                draw = draw + gather(t, lag_tile) * weight
+            moment = draw * raw * line
+            for j in range(per):
+                decay_sum = decay_sum - moment[:, j * LANES : (j + 1) * LANES]
+            dmix = split(draw * jnp.exp(-speed * line))
+            second_sum = second_sum + nt(dmix, split(basis_buf[:, pl.ds(start, long)]))
+            dbasis = product(mixer, dmix) * slope_buf[:, pl.ds(start, long)]
+            first_sum = first_sum + nt(split(embed), split(dbasis))
+            return second_sum, first_sum, decay_sum
+
+        order = basis_buf.shape[0]
+        state = (
+            jnp.zeros((padded, order), jnp.float32),
+            jnp.zeros((embed_buf.shape[0], order), jnp.float32),
+            jnp.zeros((padded, LANES), jnp.float32),
+        )
+        covered, steps = lags.shape[0] * run // per, length // long
+        state = lax.fori_loop(0, covered, functools.partial(step, True), state)
+        if covered < steps:
+            state = lax.fori_loop(covered, steps, functools.partial(step, False), state)
+        second_sum, first_sum, decay_sum = state
+        second_buf[base : base + padded] = second_sum
+        first_buf[...] = first_buf[...] + first_sum
+        decay[base : base + padded] = decay_sum
 
     second, third = (w2h[...], w2l[...]), (w3h[...], w3l[...])
     count = 2 if group % 2 == 0 else 1
@@ -352,6 +345,8 @@
                     gain = gains[pl.ds(other * padded + g * 8 + lane, 1), :]
                     put(late_cot, g, lane, group, values[j] * inverse[at, :] + gain * cots[j])
                     put(late_sig, g, lane, group, values[count + j])
+                    skip[at, :] = jnp.sum(cots[j] * sigs[j], axis=0, keepdims=True)
+                    project[at, :] = jnp.sum(raws[j] * values[count + j], axis=0, keepdims=True)
                 return carry
 
             lax.fori_loop(0, pairs, step, 0)
@@ -359,17 +354,10 @@
             for k in range(1, half):
                 to = lax.rem(own + k, half)
                 send(late_cot.at[to, g], in_out.at[own, g], late_ig_sent, ig_got, to + half)
-            pltpu.make_async_copy(late_sig.at[:, g], filt_out.at[groups + g, pl.ds(0, half)], done.at[4]).start()
-            pltpu.make_async_copy(zero_buf, filt_out.at[groups + g, pl.ds(half, half)], done.at[5]).start()
             return carry
 
         lax.fori_loop(0, groups, chunk, 0)
-
-    @pl.when(jnp.logical_not(late))
-    def _():
-        for g in range(groups):
-            pltpu.make_async_copy(zero_buf, filt_out.at[groups + g, pl.ds(0, half)], done.at[4]).start()
-            pltpu.make_async_copy(zero_buf, filt_out.at[groups + g, pl.ds(half, half)], done.at[5]).start()
+        functionals(late_sig, padded, mix_t[own][:, :padded])
 
     first, last = (w1h[...], w1l[...]), (w4h[...], w4l[...])
     cos_t, sin_t = ct[...], st[...]
@@ -427,19 +415,79 @@
             values = backward(prods, third, last, cos_t, sin_t)
             for j, lane in enumerate(lanes):
                 put(sig_buf, g, lane, group, values[j])
+                at = pl.ds(g * 8 + lane, 1)
+                raw = raw_buf[g, pl.ds(lane, rows, stride=8), :]
+                skip[at, :] = jnp.sum(cots[j] * sigs[j], axis=0, keepdims=True)
+                project[at, :] = jnp.sum(raw * values[j], axis=0, keepdims=True)
             return carry
 
         lax.fori_loop(0, pairs, step, 0)
-        pltpu.make_async_copy(sig_buf.at[:, g], filt_out.at[g], done.at[6]).start()
         return carry
 
     lax.fori_loop(0, groups, filter_chunk, 0)
 
-    for i, (src, dst) in enumerate(outputs):
-        settle(dst, done.at[i])
-    settle(filt_out.at[pl.ds(0, groups), pl.ds(0, half)], done.at[4])
-    settle(filt_out.at[pl.ds(0, groups), pl.ds(0, half)], done.at[5])
-    settle(filt_out.at[pl.ds(0, groups)], done.at[6])
+    functionals(sig_buf, 0, mix_t[me][:, :padded])
+
+    def row_of(ref):
+        column = jnp.sum(ref[...], axis=1, keepdims=True)
+        shape = (2 * padded, LANES)
+        same = lax.broadcasted_iota(jnp.int32, shape, 0) == lax.broadcasted_iota(jnp.int32, shape, 1)
+        return jnp.sum(jnp.where(same, column, 0.0), axis=0, keepdims=True)
+
+    order = basis_buf.shape[0]
+    tall = embed_buf.shape[0]
+    mine_buf[: 2 * padded, :order] = second_buf[...]
+    mine_buf[:tall, order:] = first_buf[...]
+    mine_buf[tall : tall + 1, order:] = row_of(decay)[:, :order]
+    mine_buf[tall + 1 : tall + 2, order:] = factor * row_of(skip)[:, :order]
+
+    copies = []
+    for k in range(1, parts):
+        copies.append(
+            pltpu.make_async_remote_copy(
+                src_ref=mine_buf,
+                dst_ref=slots.at[k],
+                send_sem=sends.at[k],
+                recv_sem=arrivals.at[k],
+                device_id=(lax.rem(me + k, parts), my_chan),
+                device_id_type=MESH,
+            )
+        )
+        copies[-1].start()
+    slots[0] = mine_buf[...]
+    for copy in copies:
+        copy.wait_recv()
+    acc = jnp.zeros(partial.shape, jnp.float32)
+    for b in range(parts):
+        block = slots[lax.rem(me + parts - b, parts)]
+        shared[b] = block
+        acc = acc + block[:tall]
+    partial[...] = acc
+    for copy in copies:
+        copy.wait_send()
+    copies = []
+    for k in range(1, chans):
+        copies.append(
+            pltpu.make_async_remote_copy(
+                src_ref=partial,
+                dst_ref=sums.at[k],
+                send_sem=sends2.at[k],
+                recv_sem=arrivals2.at[k],
+                device_id=(me, lax.rem(my_chan + k, chans)),
+                device_id_type=MESH,
+            )
+        )
+        copies[-1].start()
+    sums[0] = acc
+    for copy in copies:
+        copy.wait_recv()
+    acc = jnp.zeros_like(acc)
+    for c in range(chans):
+        acc = acc + sums[lax.rem(my_chan + chans - c, chans)]
+    whole[...] = acc
+    for copy in copies:
+        copy.wait_send()
+
     settle(cot_in.at[pl.ds(0, parts - 1)], cot_sent)
     settle(in_out, ig_got)
 
@@ -456,12 +504,14 @@
         settle(cot_in.at[pl.ds(0, half - 1)], ig_sent)
 
 
-def run_block(sig, cot, first_t, mix, rates, gains, group, length):
+def run_block(sig, cot, first_t, mix, mix_t, rates, gains, group, length, chans):
     parts, groups, run, _ = sig.shape
     half = parts // 2
     rows = length // LANES
     nb = (first_t.shape[1] - 8) // 2
-    order = first_t.shape[0]
+    order, tall = first_t.shape
+    both = 2 * groups * 8
+    high = -(-max(both, tall + 2) // 8) * 8
     tabs = tables(rows, LANES)
     small = tables(rows // 2, LANES)
     small = (*small[:2], *small[6:])
@@ -469,19 +519,15 @@
     vmem = pl.BlockSpec(memory_space=pltpu.VMEM)
     dma = pltpu.SemaphoreType.DMA
     f32 = jnp.float32
-    pieces = (first_t, mix, rates, gains, *tabs, *small)
+    pieces = (first_t, mix, mix_t, rates, gains, *tabs, *small)
     return pl.pallas_call(
-        functools.partial(block_kernel, parts, group, nb),
+        functools.partial(block_kernel, parts, chans, group, nb),
         in_specs=[hbm, hbm] + [vmem] * len(pieces),
-        out_specs=[hbm] * 6 + [vmem],
+        out_specs=[hbm, vmem, vmem],
         out_shape=[
             jax.ShapeDtypeStruct(sig.shape, f32),
-            jax.ShapeDtypeStruct((2 * groups, parts, run, LANES), f32),
-            jax.ShapeDtypeStruct((2 * groups, rows * 8, LANES), f32),
-            jax.ShapeDtypeStruct((order, length), f32),
-            jax.ShapeDtypeStruct((order, length), f32),
-            jax.ShapeDtypeStruct((first_t.shape[1], length), f32),
-            jax.ShapeDtypeStruct((2 * groups * 8, LANES), f32),
+            jax.ShapeDtypeStruct((parts, high, LANES), f32),
+            jax.ShapeDtypeStruct((tall, LANES), f32),
         ],
         scratch_shapes=[
             pltpu.VMEM(sig.shape, f32),
@@ -492,9 +538,17 @@
             pltpu.VMEM((2 * groups, rows * 8, LANES), f32),
             pltpu.VMEM((order, length), f32),
             pltpu.VMEM((order, length), f32),
-            pltpu.VMEM((first_t.shape[1], length), f32),
-            pltpu.VMEM((half, run, LANES), f32),
-            pltpu.VMEM((2 * groups * 8, LANES), f32),
+            pltpu.VMEM((tall, length), f32),
+            pltpu.VMEM((both, LANES), f32),
+            pltpu.VMEM((both, LANES), f32),
+            pltpu.VMEM((both, LANES), f32),
+            pltpu.VMEM((both, LANES), f32),
+            pltpu.VMEM((both, order), f32),
+            pltpu.VMEM((tall, order), f32),
+            pltpu.VMEM((high, LANES), f32),
+            pltpu.VMEM((parts, high, LANES), f32),
+            pltpu.VMEM((tall, LANES), f32),
+            pltpu.VMEM((chans, tall, LANES), f32),
             dma((groups,)),
             dma((groups,)),
             dma((groups,)),
@@ -505,7 +559,10 @@
             dma,
             dma,
             dma,
-            dma((7,)),
+            dma((parts,)),
+            dma((parts,)),
+            dma((chans,)),
+            dma((chans,)),
         ],
         compiler_params=pltpu.CompilerParams(
             collective_id=1, has_side_effects=True, vmem_limit_bytes=67043328
@@ -516,15 +573,12 @@
 
 def local(signal, cotangent, first_layer, second_layer, decay_rate, skip_gain):
     parts = lax.axis_size("batch")
-    place = lax.axis_index("batch")
     width_dev, local_len = signal.shape
     bands, order = first_layer.shape
     length = local_len * parts
-    factor = 1.0 / math.sqrt(length)
     narrow = width_dev // parts
     group = min(8, narrow)
     groups = narrow // group
-    rows = length // LANES
     nb = bands // 2
 
     def tiles(x):
@@ -539,70 +593,36 @@
     first_t = jnp.concatenate([first_layer[1:], first_layer[:1]], axis=0)
     first_t = jnp.pad(first_t, ((0, 7), (0, 0))).T
     spread = lambda x: jnp.broadcast_to(fill(x), (parts * groups * 8, LANES))
-    in_grad, filt_grad, shaped, basis, slope, embed, norms = run_block(
+    mix_t = fill(second_layer.T).reshape(parts, groups * 8, order).transpose(0, 2, 1)
+    mix_t = jnp.pad(mix_t, ((0, 0), (0, 0), (0, max(0, LANES - groups * 8))))
+    in_grad, shared, total = run_block(
         tiles(signal),
         tiles(cotangent),
         first_t,
         fill(second_layer.T),
+        mix_t,
         spread(decay_rate),
         spread(skip_gain),
         group,
         length,
+        lax.axis_size("chan"),
     )
     input_grad = in_grad.reshape(parts, groups, local_len // LANES, group, LANES)
     input_grad = input_grad.transpose(0, 1, 3, 2, 4).reshape(width_dev, local_len)
-
-    def flat(x, q):
-        x = x.reshape(2 * groups, rows, q, LANES).transpose(0, 2, 1, 3)[:, :group]
-        return x.reshape(2 * narrow, length)
-
-    other = (place + parts // 2) % parts
-
-    def both(x):
-        own = lax.dynamic_slice_in_dim(x, place * narrow, narrow, 0)
-        return jnp.concatenate([own, lax.dynamic_slice_in_dim(x, other * narrow, narrow, 0)])
-
-    columns = both(second_layer.T).T
-    rates = both(decay_rate)
-    norms = norms.reshape(2 * groups, 8, LANES)[:, :group, :1].reshape(2 * narrow, 1)
-    fraction = jnp.arange(length, dtype=jnp.int32).astype(jnp.float32) / length
-    window = jnp.exp(-rates[:, None] * fraction[None, :])
-    dfilt = factor * flat(filt_grad, group)
-    shaped = flat(shaped, 8)
-    filt = shaped / norms
-    project = jnp.sum(filt * dfilt, axis=1, keepdims=True)
-    draw = (dfilt - filt * project) / norms
-    decay_part = -jnp.sum(draw * shaped * fraction[None, :], axis=1)
-    dmix = draw * window
-    second_part = jnp.dot(dmix, basis.T, precision=precise)
-    dbasis = jnp.dot(columns, dmix, precision=precise)
-    first_part = jnp.dot(embed, (slope * dbasis).T, precision=precise)
-    skip_part = factor * jnp.sum(cotangent * signal, axis=1)
-    left = jnp.concatenate(
-        [
-            first_part[2 * nb : bands],
-            first_part[: 2 * nb],
-            jnp.pad(decay_part, (0, order - 2 * narrow))[None],
-            skip_part.reshape(-1, order),
-        ],
-        axis=0,
-    )
-    high = -(-max(left.shape[0], 2 * narrow) // 8) * 8
-    left = jnp.pad(left, ((0, high - left.shape[0]), (0, 0)))
-    right = jnp.pad(second_part, ((0, high - 2 * narrow), (0, 0)))
-    block = jnp.concatenate([left, right], axis=1)
-    shared, total = share(block, parts, lax.axis_size("chan"))
-    first_grad = total[:bands, :order]
-
-    def merge(own, late):
-        return own + jnp.roll(late, -(parts // 2), axis=0)
-
-    second_grad = merge(shared[:, :narrow, order:], shared[:, narrow : 2 * narrow, order:])
-    second_grad = second_grad.reshape(width_dev, order).T
-    decays = shared[:, bands]
-    decay_grad = merge(decays[:, :narrow], decays[:, narrow : 2 * narrow]).reshape(width_dev)
-    skip_grad = jnp.sum(shared[:, bands + 1 : bands + 1 + width_dev // order, :order], axis=0)
-    return (input_grad, first_grad, second_grad, decay_grad, skip_grad.reshape(width_dev))
+    first_grad = total[: bands + 7, order:]
+    first_grad = jnp.concatenate([first_grad[2 * nb : bands], first_grad[: 2 * nb]], axis=0)
+
+    def merge(x):
+        own, late = x[:, : groups * 8], x[:, groups * 8 : 2 * groups * 8]
+        x = own + jnp.roll(late, -(parts // 2), axis=0)
+        x = x.reshape(parts, groups, 8, *x.shape[2:])[:, :, :group]
+        return x.reshape(width_dev, *x.shape[3:])
+
+    second_grad = merge(shared[:, :, :order]).T
+    tall = bands + 7
+    decay_grad = merge(shared[:, tall, order:])
+    skip_grad = merge(shared[:, tall + 1, order:])
+    return (input_grad, first_grad, second_grad, decay_grad, skip_grad)
 
 
 def solution(mesh):

time: 325 us -> 285 us (0.88)
  other arithmetic: 33.1 us -> 2.27 us
  matrix products: 23.3 us -> 0 us
  Pallas kernels: 250 us -> 264 us
    dot_general x3 -> x0, matrix products: 23.3 us -> none  [the longest x1 10.2 us: local(): dbasis = jnp.dot(columns, dmix, precision=precise)]
    reduce_sum x4 -> x0, other arithmetic: 15.4 us -> none  [the longest x1 7.3 us: local(): decay_part = -jnp.sum(draw * shaped * fraction[None, :], axis=1)]
    mul x3 -> x0, other arithmetic: 15.1 us -> none  [the longest x1 8.09 us: local(): dfilt = factor * flat(filt_grad, group)]
    pallas_call x2 -> x1, Pallas kernels: 250 us -> 264 us  [run_block(): pl.pallas_call(functools.partial(block_kernel, parts, chans, group, nb),...]
where the time goes in v4:
time: 285 us; the launch traced here: 284 us
  Pallas kernels  264 us (93%)
  local copies, waits for them, and re-layouts  17 us (6%)
    pallas_call x1, Pallas kernels, run_block(): pl.pallas_call(functools.partial(block_kernel, parts, chans, group, nb),...  264 us
    unnamed x5, local copies, waits for them, and re-layouts  6.31 us

profile of v4, /device:TPU:0, one launch (start us, length us, event | category | flops | bytes accessed | tf_op | source)
XLA Modules:
  0.0 284.1 jit_solution(8462386623805339241)
XLA Ops:
  0.6 0.9 copy.33
  1.6 0.0 copy-start
  1.6 0.6 copy-done
  2.2 0.1 copy.34
  2.4 0.7 pad.9.mix_t
  3.1 1.4 broadcast_in_dim.4.rates
  4.5 1.4 broadcast_in_dim.5.gains
  5.9 0.7 slice.64
  6.7 0.1 copy.36
  6.8 0.7 slice.65
  7.4 0.1 copy.32
  7.5 0.7 fusion.first_t
  8.2 264.1 %block.1 = (f32[8,4,256,128]{3,2,1,0:T(8,128)}, f32[8,64,128]{2,1,0:T(8,128)}, f32[40,128]{1,0:T(8,128)}) custom-call(f32[8,4,256,128]{3,2,1,0:T(8,128)} %bitcast.26, f32[8,4,256,128]{3,2,1,0:T(8,128)} %bitcast.27, f32[64,40]{1,0:T(8,128)} %fusion.first_t, f32[256,64]{1,0:T(8,128)} %bitcast.29, f32[8,64,128]{2,1,0:T(8,128)} %pad.9.mix_t, ...), custom_call_target="tpu_custom_call" | custom-call | tf_op jit(solution)/shard_map/block/pallas_call | solution.py:523
  272.4 0.9 fusion.1
  273.3 0.1 fusion.3
  273.4 0.6 reshape_reshape.15
  274.0 0.1 fusion.4
  274.1 0.6 reshape_reshape.14
  274.8 0.9 fusion.2
  275.6 0.9 maximum_add_fusion
  276.6 0.7 copy.35
  277.3 0.8 slice.67
  278.1 0.8 slice.66
  278.8 0.6 pad_maximum_fusion
  279.4 4.7 %copy.38 = f32[256,4096]{1,0:T(8,128)} copy(f32[256,4096]{1,0:T(8,128)} %bitcast.25) | data formatting | bytes 8388608
  (2 shorter events, 0.0 us)
Async XLA Ops:
  1.6 0.7 copy-start

commit v5 on v4

--- a/solution.py
+++ b/solution.py
@@ -125,14 +125,14 @@
 
 
 def block_kernel(
-    parts, chans, group, nb, sig_in, cot_in, first_t, mix, mix_t, rates, gains,
+    parts, chans, group, nb, sig_in, cot_in, first_t, layer, rates, gains,
     w1h, w1l, w2h, w2l, w3h, w3l, w4h, w4l, ct, st,
     v1h, v1l, v4h, v4l, cv, sv,
-    in_out, shared, whole,
+    in_out, turned, lines, whole,
     cot_buf, sig_buf, ig_buf, late_cot, late_sig, raw_buf, basis_buf, slope_buf, embed_buf,
-    inverse, project, skip, decay, second_buf, first_buf, mine_buf, slots, partial, sums,
+    inverse, gain_buf, project, skip, late_msg, late_in, first_buf, mine_buf, slots, partial, sums,
     cot_got, sig_got, late_cot_got, late_sig_got, ig_got,
-    cot_sent, sig_sent, late_sent, ig_sent, late_ig_sent, sends, arrivals, sends2, arrivals2,
+    cot_sent, sig_sent, late_sent, ig_sent, late_ig_sent, msg_sent, msg_got, sends, arrivals, sends2, arrivals2,
 ):
     me, my_chan = lax.axis_index("batch"), lax.axis_index("chan")
     half = parts // 2
@@ -198,14 +198,36 @@
 
     skip[...] = jnp.zeros(skip.shape, jnp.float32)
     project[...] = jnp.zeros(project.shape, jnp.float32)
-    decay[...] = jnp.zeros(decay.shape, jnp.float32)
-    second_buf[...] = jnp.zeros(second_buf.shape, jnp.float32)
+    mine_buf[...] = jnp.zeros(mine_buf.shape, jnp.float32)
     first_buf[...] = jnp.zeros(first_buf.shape, jnp.float32)
     other = lax.rem(me + half, parts)
-    mine = pl.ds(pl.multiple_of(me * padded, 8), padded)
-    theirs = pl.ds(pl.multiple_of(other * padded, 8), padded)
-    weights = split(jnp.concatenate([mix[mine, :], mix[theirs, :]], axis=0))
-    rate = jnp.concatenate([rates[mine, :], rates[theirs, :]], axis=0)[:, :1]
+    wide = layer.shape[1]
+    nt_dims = (((1,), (1,)), ((), ()))
+
+    def pick(owner):
+        line = lax.broadcasted_iota(jnp.int32, (padded, wide), 0)
+        spot = owner * groups * group + lax.shift_right_logical(line, 3) * group + (line & 7)
+        return jnp.logical_and(
+            lax.broadcasted_iota(jnp.int32, (padded, wide), 1) == spot, (line & 7) < group
+        )
+
+    def column(mask, row):
+        return jnp.sum(jnp.where(mask, row, 0.0), axis=1, keepdims=True)
+
+    def exact_nt(left, right):
+        return lax.dot_general(
+            left, right, nt_dims, precision=exact, preferred_element_type=jnp.float32
+        )
+
+    masks = [pick(me), pick(other)]
+    hots = [mask.astype(jnp.float32) for mask in masks]
+    weights = split(jnp.concatenate([exact_nt(hot, layer[...]) for hot in hots], axis=0))
+    mixers = [split(exact_nt(layer[...], hot)) for hot in hots]
+    rate = jnp.concatenate([column(mask, rates[...]) for mask in masks], axis=0)
+    for i, mask in enumerate(masks):
+        gain_buf[i * padded : (i + 1) * padded] = jnp.broadcast_to(
+            column(mask, gains[...]), (padded, LANES)
+        )
     tile = 512 if length % 512 == 0 else LANES
     width = tile // LANES
 
@@ -242,15 +264,12 @@
     factor = 1.0 / math.sqrt(length)
     long = 1024 if length % 1024 == 0 else LANES
 
-    def total_of(ref, base):
-        return jnp.sum(ref[pl.ds(base, padded), :], axis=1, keepdims=True)
-
-    def functionals(lags, base, weights_t):
+    def functionals(lags, base, mixer, projected):
         scale = inverse[pl.ds(base, padded), :][:, :1]
         weight = factor * scale
-        shift = -weight * scale * scale * total_of(project, base)
+        if projected is not None:
+            shift = -weight * scale * scale * jnp.sum(projected, axis=1, keepdims=True)
         speed = rate[base : base + padded]
-        mixer = split(weights_t)
         per = long // LANES
         run = lags.shape[2] // group
         first_chunk = base // 8
@@ -277,19 +296,18 @@
             return raw_buf[first_chunk + h, pl.ds(pl.multiple_of(r * 8, 8), 8), :]
 
         def nt(left, right):
-            dims = (((1,), (1,)), ((), ()))
-            one = lambda x, y: lax.dot_general(x, y, dims, preferred_element_type=jnp.float32)
+            one = lambda x, y: lax.dot_general(x, y, nt_dims, preferred_element_type=jnp.float32)
             return one(left[0], right[0]) + (one(left[1], right[0]) + one(left[0], right[1]))
 
-        def step(lagged, t, sums_so_far):
+        def step(t, sums_so_far):
             second_sum, first_sum, decay_sum = sums_so_far
             start = pl.multiple_of(t * long, long)
             embed = embed_buf[:, pl.ds(start, long)]
             line = embed[2 * nb : 2 * nb + 1]
             raw = gather(t, raw_tile)
-            draw = raw * shift
-            if lagged:
-                draw = draw + gather(t, lag_tile) * weight
+            draw = gather(t, lag_tile) * weight
+            if projected is not None:
+                draw = draw + raw * shift
             moment = draw * raw * line
             for j in range(per):
                 decay_sum = decay_sum - moment[:, j * LANES : (j + 1) * LANES]
@@ -305,14 +323,7 @@
             jnp.zeros((embed_buf.shape[0], order), jnp.float32),
             jnp.zeros((padded, LANES), jnp.float32),
         )
-        covered, steps = lags.shape[0] * run // per, length // long
-        state = lax.fori_loop(0, covered, functools.partial(step, True), state)
-        if covered < steps:
-            state = lax.fori_loop(covered, steps, functools.partial(step, False), state)
-        second_sum, first_sum, decay_sum = state
-        second_buf[base : base + padded] = second_sum
-        first_buf[...] = first_buf[...] + first_sum
-        decay[base : base + padded] = decay_sum
+        return lax.fori_loop(0, lags.shape[0] * run // per, step, state)
 
     second, third = (w2h[...], w2l[...]), (w3h[...], w3l[...])
     count = 2 if group % 2 == 0 else 1
@@ -322,6 +333,7 @@
     @pl.when(late)
     def _():
         own = me - half
+        late_msg[...] = jnp.zeros(late_msg.shape, jnp.float32)
         first, last = (v1h[...], v1l[...]), (v4h[...], v4l[...])
         cos_t, sin_t = cv[...], sv[...]
 
@@ -342,11 +354,14 @@
                 values = backward(prods, third, last, cos_t, sin_t)
                 for j, lane in enumerate(lanes):
                     at = pl.ds(padded + g * 8 + lane, 1)
-                    gain = gains[pl.ds(other * padded + g * 8 + lane, 1), :]
+                    gain = gain_buf[at, :]
                     put(late_cot, g, lane, group, values[j] * inverse[at, :] + gain * cots[j])
                     put(late_sig, g, lane, group, values[count + j])
-                    skip[at, :] = jnp.sum(cots[j] * sigs[j], axis=0, keepdims=True)
-                    project[at, :] = jnp.sum(raws[j] * values[count + j], axis=0, keepdims=True)
+                    at = pl.ds(g * 8 + lane, 1)
+                    late_msg[0, at, :] = jnp.sum(
+                        raws[j] * values[count + j], axis=0, keepdims=True
+                    )
+                    late_msg[1, at, :] = jnp.sum(cots[j] * sigs[j], axis=0, keepdims=True)
                 return carry
 
             lax.fori_loop(0, pairs, step, 0)
@@ -357,7 +372,12 @@
             return carry
 
         lax.fori_loop(0, groups, chunk, 0)
-        functionals(late_sig, padded, mix_t[own][:, :padded])
+        second_sum, first_sum, decay_sum = functionals(late_sig, padded, mixers[1], None)
+        late_msg[2] = decay_sum
+        late_msg[3, :, : second_sum.shape[1]] = second_sum
+        first_buf[...] = first_sum
+        late_in[...] = jnp.zeros(late_in.shape, jnp.float32)
+        send(late_msg, late_in, msg_sent, msg_got, own)
 
     first, last = (w1h[...], w1l[...]), (w4h[...], w4l[...])
     cos_t, sin_t = ct[...], st[...]
@@ -373,7 +393,7 @@
             prods = [conjugate(specs[j], specs[count + j]) for j in range(count)]
             values = backward(prods, third, last, cos_t, sin_t)
             for j, lane in enumerate(lanes):
-                gain = gains[pl.ds(me * padded + g * 8 + lane, 1), :]
+                gain = gain_buf[pl.ds(g * 8 + lane, 1), :]
                 scale = inverse[pl.ds(g * 8 + lane, 1), :]
                 put(ig_buf, g, lane, group, values[j] * scale + gain * cots[j])
             return carry
@@ -426,20 +446,26 @@
 
     lax.fori_loop(0, groups, filter_chunk, 0)
 
-    functionals(sig_buf, 0, mix_t[me][:, :padded])
-
-    def row_of(ref):
-        column = jnp.sum(ref[...], axis=1, keepdims=True)
-        shape = (2 * padded, LANES)
+    @pl.when(jnp.logical_not(late))
+    def _():
+        settle(late_in, msg_got)
+
+    second_sum, first_sum, decay_sum = functionals(
+        sig_buf, 0, mixers[0], project[...] + late_in[0]
+    )
+
+    def row_of(value):
+        value = jnp.sum(value, axis=1, keepdims=True)
+        shape = (padded, LANES)
         same = lax.broadcasted_iota(jnp.int32, shape, 0) == lax.broadcasted_iota(jnp.int32, shape, 1)
-        return jnp.sum(jnp.where(same, column, 0.0), axis=0, keepdims=True)
+        return jnp.sum(jnp.where(same, value, 0.0), axis=0, keepdims=True)
 
     order = basis_buf.shape[0]
     tall = embed_buf.shape[0]
-    mine_buf[: 2 * padded, :order] = second_buf[...]
-    mine_buf[:tall, order:] = first_buf[...]
-    mine_buf[tall : tall + 1, order:] = row_of(decay)[:, :order]
-    mine_buf[tall + 1 : tall + 2, order:] = factor * row_of(skip)[:, :order]
+    mine_buf[:padded, :order] = second_sum + late_in[3, :, :order]
+    mine_buf[:tall, order:] = first_sum + first_buf[...]
+    mine_buf[padded : padded + 1, :order] = row_of(decay_sum + late_in[2])[:, :order]
+    mine_buf[padded + 1 : padded + 2, :order] = factor * row_of(skip[...] + late_in[1])[:, :order]
 
     copies = []
     for k in range(1, parts):
@@ -458,9 +484,11 @@
     for copy in copies:
         copy.wait_recv()
     acc = jnp.zeros(partial.shape, jnp.float32)
+    blocks = []
     for b in range(parts):
         block = slots[lax.rem(me + parts - b, parts)]
-        shared[b] = block
+        blocks.append(block[:padded])
+        lines[b] = block[padded : padded + 8]
         acc = acc + block[:tall]
     partial[...] = acc
     for copy in copies:
@@ -479,6 +507,7 @@
         )
         copies[-1].start()
     sums[0] = acc
+    turned[...] = jnp.concatenate(blocks, axis=0).T[:order]
     for copy in copies:
         copy.wait_recv()
     acc = jnp.zeros_like(acc)
@@ -495,6 +524,7 @@
     def _():
         settle(cot_in.at[pl.ds(0, 2 * (half - 1))], late_sent)
         settle(cot_in.at[pl.ds(0, half - 1)], late_ig_sent)
+        settle(late_msg, msg_sent)
         settle(cot_in.at[pl.ds(0, half - 1)], sig_sent)
         settle(cot_in.at[pl.ds(0, parts - 1)], ig_sent)
 
@@ -504,14 +534,14 @@
         settle(cot_in.at[pl.ds(0, half - 1)], ig_sent)
 
 
-def run_block(sig, cot, first_t, mix, mix_t, rates, gains, group, length, chans):
+def run_block(sig, cot, first_t, layer, rates, gains, group, length, chans):
     parts, groups, run, _ = sig.shape
     half = parts // 2
     rows = length // LANES
     nb = (first_t.shape[1] - 8) // 2
     order, tall = first_t.shape
-    both = 2 * groups * 8
-    high = -(-max(both, tall + 2) // 8) * 8
+    padded = groups * 8
+    high = max(-(-tall // 8) * 8, padded + 8)
     tabs = tables(rows, LANES)
     small = tables(rows // 2, LANES)
     small = (*small[:2], *small[6:])
@@ -519,14 +549,15 @@
     vmem = pl.BlockSpec(memory_space=pltpu.VMEM)
     dma = pltpu.SemaphoreType.DMA
     f32 = jnp.float32
-    pieces = (first_t, mix, mix_t, rates, gains, *tabs, *small)
+    pieces = (first_t, layer, rates, gains, *tabs, *small)
     return pl.pallas_call(
         functools.partial(block_kernel, parts, chans, group, nb),
         in_specs=[hbm, hbm] + [vmem] * len(pieces),
-        out_specs=[hbm, vmem, vmem],
+        out_specs=[hbm, vmem, vmem, vmem],
         out_shape=[
             jax.ShapeDtypeStruct(sig.shape, f32),
-            jax.ShapeDtypeStruct((parts, high, LANES), f32),
+            jax.ShapeDtypeStruct((order, parts * padded), f32),
+            jax.ShapeDtypeStruct((parts, 8, LANES), f32),
             jax.ShapeDtypeStruct((tall, LANES), f32),
         ],
         scratch_shapes=[
@@ -539,11 +570,12 @@
             pltpu.VMEM((order, length), f32),
             pltpu.VMEM((order, length), f32),
             pltpu.VMEM((tall, length), f32),
-            pltpu.VMEM((both, LANES), f32),
-            pltpu.VMEM((both, LANES), f32),
-            pltpu.VMEM((both, LANES), f32),
-            pltpu.VMEM((both, LANES), f32),
-            pltpu.VMEM((both, order), f32),
+            pltpu.VMEM((2 * padded, LANES), f32),
+            pltpu.VMEM((2 * padded, LANES), f32),
+            pltpu.VMEM((padded, LANES), f32),
+            pltpu.VMEM((padded, LANES), f32),
+            pltpu.VMEM((4, padded, LANES), f32),
+            pltpu.VMEM((4, padded, LANES), f32),
             pltpu.VMEM((tall, order), f32),
             pltpu.VMEM((high, LANES), f32),
             pltpu.VMEM((parts, high, LANES), f32),
@@ -553,6 +585,8 @@
             dma((groups,)),
             dma((groups,)),
             dma((groups,)),
+            dma,
+            dma,
             dma,
             dma,
             dma,
@@ -585,24 +619,15 @@
         x = x.reshape(parts, groups, group, local_len // LANES, LANES)
         return x.transpose(0, 1, 3, 2, 4).reshape(parts, groups, -1, LANES)
 
-    def fill(x):
-        x = x.reshape(parts * groups, group, -1)
-        x = jnp.pad(x, ((0, 0), (0, 8 - group), (0, 0)))
-        return x.reshape(parts * groups * 8, -1)
-
     first_t = jnp.concatenate([first_layer[1:], first_layer[:1]], axis=0)
     first_t = jnp.pad(first_t, ((0, 7), (0, 0))).T
-    spread = lambda x: jnp.broadcast_to(fill(x), (parts * groups * 8, LANES))
-    mix_t = fill(second_layer.T).reshape(parts, groups * 8, order).transpose(0, 2, 1)
-    mix_t = jnp.pad(mix_t, ((0, 0), (0, 0), (0, max(0, LANES - groups * 8))))
-    in_grad, shared, total = run_block(
+    in_grad, turned, lines, total = run_block(
         tiles(signal),
         tiles(cotangent),
         first_t,
-        fill(second_layer.T),
-        mix_t,
-        spread(decay_rate),
-        spread(skip_gain),
+        second_layer,
+        decay_rate.reshape(1, -1),
+        skip_gain.reshape(1, -1),
         group,
         length,
         lax.axis_size("chan"),
@@ -612,16 +637,13 @@
     first_grad = total[: bands + 7, order:]
     first_grad = jnp.concatenate([first_grad[2 * nb : bands], first_grad[: 2 * nb]], axis=0)
 
-    def merge(x):
-        own, late = x[:, : groups * 8], x[:, groups * 8 : 2 * groups * 8]
-        x = own + jnp.roll(late, -(parts // 2), axis=0)
-        x = x.reshape(parts, groups, 8, *x.shape[2:])[:, :, :group]
-        return x.reshape(width_dev, *x.shape[3:])
-
-    second_grad = merge(shared[:, :, :order]).T
-    tall = bands + 7
-    decay_grad = merge(shared[:, tall, order:])
-    skip_grad = merge(shared[:, tall + 1, order:])
+    def kept(x):
+        x = x.reshape(-1, parts * groups, 8)[:, :, :group]
+        return x.reshape(-1, width_dev)
+
+    second_grad = kept(turned) if group < 8 else turned
+    rest = kept(lines[:, :2, : groups * 8].transpose(1, 0, 2))
+    decay_grad, skip_grad = rest[0], rest[1]
     return (input_grad, first_grad, second_grad, decay_grad, skip_grad)
 
 

time: 285 us -> 266 us (0.933)
  Pallas kernels: 264 us -> 253 us
  local copies, waits for them, and re-layouts: 17 us -> 10.5 us
    pallas_call x1, Pallas kernels: 264 us -> 253 us  [run_block(): pl.pallas_call(functools.partial(block_kernel, parts, chans, group, nb),...]
    broadcast_in_dim x2 -> x0, local copies, waits for them, and re-layouts: 2.85 us -> none  [local(): spread = lambda x: jnp.broadcast_to(fill(x), (parts * groups * 8, LANES))]
where the time goes in v5:
time: 266 us
  Pallas kernels  253 us (95%)
  local copies, waits for them, and re-layouts  10.5 us (4%)
    pallas_call x1, Pallas kernels, run_block(): pl.pallas_call(functools.partial(block_kernel, parts, chans, group, nb),...  253 us
    unnamed x5, local copies, waits for them, and re-layouts  5.4 us

profile of v5, /device:TPU:0, one launch (start us, length us, event | category | flops | bytes accessed | tf_op | source)
XLA Modules:
  0.0 265.9 jit_solution(7860404738958005043)
XLA Ops:
  0.6 0.7 slice.26
  1.4 0.1 copy.29
  1.4 0.7 slice.27
  2.1 0.1 copy.28
  2.2 0.7 fusion.first_t
  2.9 253.4 %block.1 = (f32[8,4,256,128]{3,2,1,0:T(8,128)}, f32[64,256]{1,0:T(8,128)}, f32[8,8,128]{2,1,0:T(8,128)}, f32[40,128]{1,0:T(8,128)}) custom-call(f32[8,4,256,128]{3,2,1,0:T(8,128)} %bitcast.21, f32[8,4,256,128]{3,2,1,0:T(8,128)} %bitcast.22, f32[64,40]{1,0:T(8,128)} %fusion.first_t, f32[64,256]{1,0:T(8,128)} %layer.1, f32[1,256]{1,0:T(1,128)} %bitcast.24, ...), custom_call_target="tpu_custom_call" | custom-call | tf_op jit(solution)/shard_map/block/pallas_call | solution.py:553
  256.4 0.8 slice.29
  257.2 0.8 slice.28
  257.9 0.6 pad_maximum_fusion
  258.6 0.8 slice_bitcast_fusion
  259.3 0.6 squeeze.6
  260.0 0.6 squeeze.7
  260.6 0.0 copy-start
  260.6 4.7 %copy.32 = f32[256,4096]{1,0:T(8,128)} copy(f32[256,4096]{1,0:T(8,128)} %bitcast.23) | data formatting | bytes 8388608
  265.3 0.0 copy-done
  265.3 0.6 copy.33
  (1 shorter events, 0.0 us)
Async XLA Ops:
  260.6 4.7 %copy-start = (f32[64,256]{1,0:T(8,128)S(1)}, f32[64,256]{1,0:T(8,128)}, u32[]{:S(2)}) copy-start(f32[64,256]{1,0:T(8,128)} %get-tuple-element.22) | copy-start | bytes 196612
